TPU v7x, 32 devices: a 4x2x2 block of a 4x4x8 slice. The times are simulated.
32 devices in a mesh: dp: 4 (over y, z), tp: 8 (over x, core).
Axes of the slice: x: 4, y: 2, z: 2, core: 2. Of those that a mesh axis runs over, the one named last changes fastest.
The devices are a block of a 4x4x8 slice.
Arguments:
- x_in: bfloat16 [2, 1024, 2048], P(None, ('dp', 'tp')), parts along dimension 1
- y_cot: bfloat16 [2, 1024, 2048], P(None, ('dp', 'tp')), parts along dimension 1
- gain_attn: float32 [2, 2048], replicated
- gain_mlp: float32 [2, 2048], replicated
- w_qkv: bfloat16 [2, 2048, 8, 4, 128], P(None, None, 'tp')
- w_out: bfloat16 [2, 16, 128, 2048], P(None, 'tp')
- w_gate: bfloat16 [2, 2048, 6144], P(None, None, 'tp')
- w_up: bfloat16 [2, 2048, 6144], P(None, None, 'tp')
- w_down: bfloat16 [2, 6144, 2048], P(None, 'tp')
Outputs:
- output 1: bfloat16 [2, 1024, 2048], P(None, ('dp', 'tp')), parts along dimension 1
- output 2: bfloat16 [2, 1024, 2048], P(None, ('dp', 'tp')), parts along dimension 1
- output 3: bfloat16 [8, 2048, 8, 4, 128], P('dp', None, 'tp'), parts along dimension 0
- output 4: bfloat16 [8, 16, 128, 2048], P('dp', 'tp'), parts along dimension 0
- output 5: bfloat16 [8, 2048, 6144], P('dp', None, 'tp'), parts along dimension 0
- output 6: bfloat16 [8, 2048, 6144], P('dp', None, 'tp'), parts along dimension 0
- output 7: bfloat16 [8, 6144, 2048], P('dp', 'tp'), parts along dimension 0
- output 8: float32 [8, 2048], P('dp'), parts along dimension 0
- output 9: float32 [8, 2048], P('dp'), parts along dimension 0
There are 4 independent parts. A program takes and returns all parts, laid end to end along the dimension named above; an argument that names none is the same for every part.
All inputs are finite; a program needn't handle non-finite values.
Results may differ from a plain program's by a relative error of at most 0.02.
Values are sent between devices in bfloat16 or wider.
A program may use at most 768 MiB of HBM per device.

v0:
```python
import jax
import jax.numpy as jnp
from jax import lax
from jax.sharding import PartitionSpec as P

NORM_EPS = 1e-5


def rms_scale(row_vals, gain_vec):
    return row_vals * lax.rsqrt(jnp.mean(row_vals * row_vals, axis=-1, keepdims=True) + NORM_EPS) * gain_vec


def norm_apply(row_vals, gain_vec):
    return rms_scale(row_vals.astype(jnp.float32), gain_vec).astype(jnp.bfloat16)


def norm_backward(row_vals, gain_vec, cot_rows):
    unused, pull = jax.vjp(rms_scale, row_vals.astype(jnp.float32), gain_vec)
    return pull(cot_rows.astype(jnp.float32))


def causal_mask(seq_len):
    row_pos = lax.broadcasted_iota(jnp.int32, (seq_len, 1, seq_len), 0)
    col_pos = lax.broadcasted_iota(jnp.int32, (seq_len, 1, seq_len), 2)
    return row_pos >= col_pos


def attention_forward(queries, key_heads, value_heads, score_scale):
    seq_len = queries.shape[0]
    scores = jnp.einsum('qkge,tke->kqgt', queries, key_heads, preferred_element_type=jnp.float32) * score_scale
    scores = jnp.where(causal_mask(seq_len), scores, -1e30)
    row_max = jnp.max(scores, axis=-1, keepdims=True)
    exp_scores = jnp.exp(scores - row_max)
    row_total = jnp.sum(exp_scores, axis=-1, keepdims=True)
    prob_b16 = (exp_scores / row_total).astype(jnp.bfloat16)
    attn_mix = jnp.einsum('kqgt,tke->kqge', prob_b16, value_heads, preferred_element_type=jnp.float32).astype(jnp.bfloat16)
    return attn_mix, row_max + jnp.log(row_total)


def attention_backward(queries, key_heads, value_heads, log_norm, grad_mix, score_scale):
    seq_len = queries.shape[0]
    scores = jnp.einsum('qkge,tke->kqgt', queries, key_heads, preferred_element_type=jnp.float32) * score_scale
    scores = jnp.where(causal_mask(seq_len), scores, -1e30)
    prob_f32 = jnp.exp(scores - log_norm)
    prob_b16 = prob_f32.astype(jnp.bfloat16)
    grad_prob = jnp.einsum('qkge,tke->kqgt', grad_mix, value_heads, preferred_element_type=jnp.float32).astype(jnp.bfloat16).astype(jnp.float32)
    row_dot = jnp.sum(grad_prob * prob_f32, axis=-1, keepdims=True)
    grad_scores = (prob_f32 * (grad_prob - row_dot) * score_scale).astype(jnp.bfloat16)
    grad_q = jnp.einsum('kqgt,tke->qkge', grad_scores, key_heads, preferred_element_type=jnp.float32)
    grad_k = jnp.einsum('kqgt,qkge->tke', grad_scores, queries, preferred_element_type=jnp.float32)
    grad_v = jnp.einsum('kqgt,qkge->tke', prob_b16, grad_mix, preferred_element_type=jnp.float32)
    return grad_q, grad_k, grad_v


def solution(mesh):
    row_spec = P(None, ('dp', 'tp'), None)
    gain_spec = P(None, None)
    qkv_spec = P(None, None, 'tp', None, None)
    head_spec = P(None, 'tp', None, None)
    col_spec = P(None, None, 'tp')
    row_shard_spec = P(None, 'tp', None)

    def device_program(x_in, y_cot, gain_attn, gain_mlp, w_qkv, w_out, w_gate, w_up, w_down):
        micro_count = x_in.shape[0]
        width = x_in.shape[2]
        layer_count = w_qkv.shape[0]
        kv_local = w_qkv.shape[2]
        groups = w_qkv.shape[3] - 2
        head_dim = w_qkv.shape[4]
        score_scale = head_dim ** -0.5
        kept_acts = []
        y_rows = []
        for micro_idx in range(micro_count):
            layer_in = x_in[micro_idx]
            per_layer = []
            for layer_idx in range(layer_count):
                normed = norm_apply(layer_in, gain_attn[layer_idx])
                normed_full = lax.all_gather(normed, 'tp', axis=0, tiled=True)
                qkv_heads = jnp.einsum('sd,dkje->skje', normed_full, w_qkv[layer_idx], preferred_element_type=jnp.float32).astype(jnp.bfloat16)
                queries = qkv_heads[:, :, :groups]
                key_heads = qkv_heads[:, :, groups]
                value_heads = qkv_heads[:, :, groups + 1]
                attn_mix, log_norm = attention_forward(queries, key_heads, value_heads, score_scale)
                heads_out = w_out[layer_idx].reshape(kv_local, groups, head_dim, width)
                attn_part = jnp.einsum('kqge,kged->qd', attn_mix, heads_out, preferred_element_type=jnp.float32)
                attn_sum = lax.psum_scatter(attn_part, 'tp', scatter_dimension=0, tiled=True).astype(jnp.bfloat16)
                hidden = (layer_in.astype(jnp.float32) + attn_sum.astype(jnp.float32)).astype(jnp.bfloat16)
                normed_b = norm_apply(hidden, gain_mlp[layer_idx])
                normed_b_full = lax.all_gather(normed_b, 'tp', axis=0, tiled=True)
                gate_pre = jnp.dot(normed_b_full, w_gate[layer_idx], preferred_element_type=jnp.float32)
                up_proj = jnp.dot(normed_b_full, w_up[layer_idx], preferred_element_type=jnp.float32)
                inner = (jax.nn.silu(gate_pre) * up_proj).astype(jnp.bfloat16)
                down_part = jnp.dot(inner, w_down[layer_idx], preferred_element_type=jnp.float32)
                mlp_sum = lax.psum_scatter(down_part, 'tp', scatter_dimension=0, tiled=True).astype(jnp.bfloat16)
                per_layer.append((layer_in, normed, hidden, normed_b, queries, key_heads, value_heads, attn_mix, log_norm))
                layer_in = (hidden.astype(jnp.float32) + mlp_sum.astype(jnp.float32)).astype(jnp.bfloat16)
            kept_acts.append(per_layer)
            y_rows.append(layer_in)

        grad_qkv_acc = [None] * layer_count
        grad_out_acc = [None] * layer_count
        grad_gate_acc = [None] * layer_count
        grad_up_acc = [None] * layer_count
        grad_down_acc = [None] * layer_count
        gain_a_acc = [None] * layer_count
        gain_b_acc = [None] * layer_count

        def accumulate(acc_list, layer_idx, term):
            acc_list[layer_idx] = term if acc_list[layer_idx] is None else acc_list[layer_idx] + term

        grad_rows = []
        for micro_idx in range(micro_count):
            grad_in = y_cot[micro_idx]
            for layer_idx in reversed(range(layer_count)):
                layer_in, normed, hidden, normed_b, queries, key_heads, value_heads, attn_mix, log_norm = kept_acts[micro_idx][layer_idx]
                normed_b_full = lax.all_gather(normed_b, 'tp', axis=0, tiled=True)
                grad_full = lax.all_gather(grad_in, 'tp', axis=0, tiled=True)
                gate_pre = jnp.dot(normed_b_full, w_gate[layer_idx], preferred_element_type=jnp.float32)
                up_proj = jnp.dot(normed_b_full, w_up[layer_idx], preferred_element_type=jnp.float32)
                gate_sig = jax.nn.sigmoid(gate_pre)
                gate_act = gate_pre * gate_sig
                inner = (gate_act * up_proj).astype(jnp.bfloat16)
                accumulate(grad_down_acc, layer_idx, jnp.einsum('sf,sd->fd', inner, grad_full, preferred_element_type=jnp.float32))
                grad_inner = jnp.einsum('sd,fd->sf', grad_full, w_down[layer_idx], preferred_element_type=jnp.float32).astype(jnp.bfloat16).astype(jnp.float32)
                grad_up = (grad_inner * gate_act).astype(jnp.bfloat16)
                grad_gate = (grad_inner * up_proj * gate_sig * (1.0 + gate_pre * (1.0 - gate_sig))).astype(jnp.bfloat16)
                accumulate(grad_gate_acc, layer_idx, jnp.einsum('sd,sf->df', normed_b_full, grad_gate, preferred_element_type=jnp.float32))
                accumulate(grad_up_acc, layer_idx, jnp.einsum('sd,sf->df', normed_b_full, grad_up, preferred_element_type=jnp.float32))
                grad_nb_part = jnp.einsum('sf,df->sd', grad_gate, w_gate[layer_idx], preferred_element_type=jnp.float32) + jnp.einsum('sf,df->sd', grad_up, w_up[layer_idx], preferred_element_type=jnp.float32)
                grad_nb = lax.psum_scatter(grad_nb_part, 'tp', scatter_dimension=0, tiled=True).astype(jnp.bfloat16)
                grad_h_norm, grad_gain_b = norm_backward(hidden, gain_mlp[layer_idx], grad_nb)
                accumulate(gain_b_acc, layer_idx, grad_gain_b)
                grad_hidden = (grad_in.astype(jnp.float32) + grad_h_norm).astype(jnp.bfloat16)
                normed_full = lax.all_gather(normed, 'tp', axis=0, tiled=True)
                grad_hfull = lax.all_gather(grad_hidden, 'tp', axis=0, tiled=True)
                heads_out = w_out[layer_idx].reshape(kv_local, groups, head_dim, width)
                accumulate(grad_out_acc, layer_idx, jnp.einsum('kqge,qd->kged', attn_mix, grad_hfull, preferred_element_type=jnp.float32).reshape(w_out.shape[1:]))
                grad_mix = jnp.einsum('qd,kged->qkge', grad_hfull, heads_out, preferred_element_type=jnp.float32).astype(jnp.bfloat16)
                grad_q, grad_k, grad_v = attention_backward(queries, key_heads, value_heads, log_norm, grad_mix, score_scale)
                grad_qkv = jnp.concatenate([grad_q, grad_k[:, :, None], grad_v[:, :, None]], axis=2).astype(jnp.bfloat16)
                accumulate(grad_qkv_acc, layer_idx, jnp.einsum('sd,skje->dkje', normed_full, grad_qkv, preferred_element_type=jnp.float32))
                grad_n_part = jnp.einsum('skje,dkje->sd', grad_qkv, w_qkv[layer_idx], preferred_element_type=jnp.float32)
                grad_n = lax.psum_scatter(grad_n_part, 'tp', scatter_dimension=0, tiled=True).astype(jnp.bfloat16)
                grad_x_norm, grad_gain_a = norm_backward(layer_in, gain_attn[layer_idx], grad_n)
                accumulate(gain_a_acc, layer_idx, grad_gain_a)
                grad_in = (grad_hidden.astype(jnp.float32) + grad_x_norm).astype(jnp.bfloat16)
            grad_rows.append(grad_in)

        gain_grads = lax.psum(jnp.stack([jnp.stack(gain_a_acc), jnp.stack(gain_b_acc)]), 'tp')
        return (jnp.stack(y_rows), jnp.stack(grad_rows),
                jnp.stack([item.astype(jnp.bfloat16) for item in grad_qkv_acc]),
                jnp.stack([item.astype(jnp.bfloat16) for item in grad_out_acc]),
                jnp.stack([item.astype(jnp.bfloat16) for item in grad_gate_acc]),
                jnp.stack([item.astype(jnp.bfloat16) for item in grad_up_acc]),
                jnp.stack([item.astype(jnp.bfloat16) for item in grad_down_acc]),
                gain_grads[0], gain_grads[1])

    return jax.shard_map(device_program, mesh=mesh,
                         in_specs=(row_spec, row_spec, gain_spec, gain_spec, qkv_spec, head_spec, col_spec, col_spec, row_shard_spec),
                         out_specs=(row_spec, row_spec, P('dp', None, 'tp', None, None), P('dp', 'tp', None, None), P('dp', None, 'tp'), P('dp', None, 'tp'), P('dp', 'tp', None), P('dp', None), P('dp', None)),
                         check_vma=False)
```

profile of v0, /device:TPU:81, one launch (start us, length us, event | category | flops | bytes accessed | tf_op | source)
XLA Modules:
  0.0 946.6 jit_solution(12407057444182295457)
XLA Ops:
  16.7 19.7 %all-gather.19.cloned.1.call-done = bf16[256,2048]{1,0:T(8,128)(2,1)} async-done(((bf16[32,2048]{1,0:T(8,128)(2,1)}), bf16[256,2048]{1,0:T(8,128)(2,1)}) %all-gather.19.cloned.1.call-update) | async-done | bytes 1048592 | tf_op jit(solution)/shard_map/all_gather | solution.py:78
  65.1 23.4 %reduce-scatter.17.cloned.1.call-done = f32[32,2048]{1,0:T(8,128)} async-done(((f32[256,2048]{1,0:T(8,128)}), f32[32,2048]{1,0:T(8,128)}) %reduce-scatter.17.cloned.1.call-update) | async-done | bytes 262160 | tf_op jit(solution)/shard_map/reduce_scatter | solution.py:86
  88.6 32.4 %reduce-scatter.25.cloned.1.call-done = f32[32,2048]{1,0:T(8,128)} async-done(((f32[256,2048]{1,0:T(8,128)}), f32[32,2048]{1,0:T(8,128)}) %reduce-scatter.25.cloned.1.call-update) | async-done | bytes 262160 | tf_op jit(solution)/shard_map/reduce_scatter | solution.py:86
  124.4 21.6 %all-gather.21.cloned.1.call-done = bf16[256,2048]{1,0:T(8,128)(2,1)} async-done(((bf16[32,2048]{1,0:T(8,128)(2,1)}), bf16[256,2048]{1,0:T(8,128)(2,1)}) %all-gather.21.cloned.1.call-update) | async-done | bytes 1048592 | tf_op jit(solution)/shard_map/all_gather | solution.py:89
  178.7 19.4 %reduce-scatter.19.cloned.1.call-done = f32[32,2048]{1,0:T(8,128)} async-done(((f32[256,2048]{1,0:T(8,128)}), f32[32,2048]{1,0:T(8,128)}) %reduce-scatter.19.cloned.1.call-update) | async-done | bytes 262160 | tf_op jit(solution)/shard_map/reduce_scatter | solution.py:94
  200.9 29.8 %reduce-scatter.27.cloned.1.call-done = f32[32,2048]{1,0:T(8,128)} async-done(((f32[256,2048]{1,0:T(8,128)}), f32[32,2048]{1,0:T(8,128)}) %reduce-scatter.27.cloned.1.call-update) | async-done | bytes 262160 | tf_op jit(solution)/shard_map/reduce_scatter | solution.py:94
  234.5 22.1 %all-gather.23.cloned.1.call-done = bf16[256,2048]{1,0:T(8,128)(2,1)} async-done(((bf16[32,2048]{1,0:T(8,128)(2,1)}), bf16[256,2048]{1,0:T(8,128)(2,1)}) %all-gather.23.cloned.1.call-update) | async-done | bytes 1048592 | tf_op jit(solution)/shard_map/all_gather | solution.py:78
  265.6 24.6 %reduce-scatter.21.cloned.1.call-done = f32[32,2048]{1,0:T(8,128)} async-done(((f32[256,2048]{1,0:T(8,128)}), f32[32,2048]{1,0:T(8,128)}) %reduce-scatter.21.cloned.1.call-update) | async-done | bytes 262160 | tf_op jit(solution)/shard_map/reduce_scatter | solution.py:86
  293.4 21.3 %all-gather.31.cloned.1.call-done = bf16[256,2048]{1,0:T(8,128)(2,1)} async-done(((bf16[32,2048]{1,0:T(8,128)(2,1)}), bf16[256,2048]{1,0:T(8,128)(2,1)}) %all-gather.31.cloned.1.call-update) | async-done | bytes 1048592 | tf_op jit(solution)/shard_map/all_gather | solution.py:78
  340.8 17.4 %all-gather.25.cloned.1.call-done = bf16[256,2048]{1,0:T(8,128)(2,1)} async-done(((bf16[32,2048]{1,0:T(8,128)(2,1)}), bf16[256,2048]{1,0:T(8,128)(2,1)}) %all-gather.25.cloned.1.call-update) | async-done | bytes 1048592 | tf_op jit(solution)/shard_map/all_gather | solution.py:89
  372.3 15.7 %reduce-scatter.29.cloned.1.call-done = f32[32,2048]{1,0:T(8,128)} async-done(((f32[256,2048]{1,0:T(8,128)}), f32[32,2048]{1,0:T(8,128)}) %reduce-scatter.29.cloned.1.call-update) | async-done | bytes 262160 | tf_op jit(solution)/shard_map/reduce_scatter | solution.py:86
  391.0 29.4 %reduce-scatter.33.cloned.1.call-done = f32[32,2048]{1,0:T(8,128)} async-done(((f32[256,2048]{1,0:T(8,128)}), f32[32,2048]{1,0:T(8,128)}) %reduce-scatter.33.cloned.1.call-update) | async-done | bytes 262160 | tf_op jit(solution)/shard_map/reduce_scatter | solution.py:130
  423.5 20.7 %all-gather.49.cloned.1.call-done = bf16[1,256,2048]{2,1,0:T(8,128)(2,1)} async-done(((bf16[1,32,2048]{2,1,0:T(8,128)(2,1)}), bf16[1,256,2048]{2,1,0:T(8,128)(2,1)}) %all-gather.49.cloned.1.call-update) | async-done | bytes 1048592 | tf_op jit(solution)/shard_map/all_gather | solution.py:117
  448.3 17.8 %all-gather.33.cloned.1.call-done = bf16[256,2048]{1,0:T(8,128)(2,1)} async-done(((bf16[32,2048]{1,0:T(8,128)(2,1)}), bf16[256,2048]{1,0:T(8,128)(2,1)}) %all-gather.33.cloned.1.call-update) | async-done | bytes 1048592 | tf_op jit(solution)/shard_map/all_gather | solution.py:89
  489.8 17.2 %reduce-scatter.41.cloned.1.call-done = f32[32,2048]{1,0:T(8,128)} async-done(((f32[256,2048]{1,0:T(8,128)}), f32[32,2048]{1,0:T(8,128)}) %reduce-scatter.41.cloned.1.call-update) | async-done | bytes 262160 | tf_op jit(solution)/shard_map/reduce_scatter | solution.py:130
  510.0 29.6 %reduce-scatter.23.cloned.1.call-done = f32[32,2048]{1,0:T(8,128)} async-done(((f32[256,2048]{1,0:T(8,128)}), f32[32,2048]{1,0:T(8,128)}) %reduce-scatter.23.cloned.1.call-update) | async-done | bytes 262160 | tf_op jit(solution)/shard_map/reduce_scatter | solution.py:94
  539.6 32.4 %reduce-scatter.31.cloned.1.call-done = f32[32,2048]{1,0:T(8,128)} async-done(((f32[256,2048]{1,0:T(8,128)}), f32[32,2048]{1,0:T(8,128)}) %reduce-scatter.31.cloned.1.call-update) | async-done | bytes 262160 | tf_op jit(solution)/shard_map/reduce_scatter | solution.py:94
  576.0 20.8 %all-gather.35.cloned.1.call-done = bf16[256,2048]{1,0:T(8,128)(2,1)} async-done(((bf16[32,2048]{1,0:T(8,128)(2,1)}), bf16[256,2048]{1,0:T(8,128)(2,1)}) %all-gather.35.cloned.1.call-update) | async-done | bytes 1048592 | tf_op jit(solution)/shard_map/all_gather | solution.py:135
  648.3 32.4 %reduce-scatter.43.cloned.1.call-done = f32[32,2048]{1,0:T(8,128)} async-done(((f32[256,2048]{1,0:T(8,128)}), f32[32,2048]{1,0:T(8,128)}) %reduce-scatter.43.cloned.1.call-update) | async-done | bytes 262160 | tf_op jit(solution)/shard_map/reduce_scatter | solution.py:143
  687.0 21.6 %all-gather.37.cloned.1.call-done = bf16[256,2048]{1,0:T(8,128)(2,1)} async-done(((bf16[32,2048]{1,0:T(8,128)(2,1)}), bf16[256,2048]{1,0:T(8,128)(2,1)}) %all-gather.37.cloned.1.call-update) | async-done | bytes 1048592 | tf_op jit(solution)/shard_map/all_gather | solution.py:117
  742.1 18.3 %reduce-scatter.37.cloned.1.call-done = f32[32,2048]{1,0:T(8,128)} async-done(((f32[256,2048]{1,0:T(8,128)}), f32[32,2048]{1,0:T(8,128)}) %reduce-scatter.37.cloned.1.call-update) | async-done | bytes 262160 | tf_op jit(solution)/shard_map/reduce_scatter | solution.py:130
  760.4 32.5 %reduce-scatter.45.cloned.1.call-done = f32[32,2048]{1,0:T(8,128)} async-done(((f32[256,2048]{1,0:T(8,128)}), f32[32,2048]{1,0:T(8,128)}) %reduce-scatter.45.cloned.1.call-update) | async-done | bytes 262160 | tf_op jit(solution)/shard_map/reduce_scatter | solution.py:130
  890.6 20.5 %copy.60 = bf16[2,2048,1,4,128]{4,3,2,1,0:T(4,128)(2,1)} copy(bf16[2,2048,1,4,128]{4,1,3,2,0:T(8,128)(2,1)S(1)} %pad_maximum_fusion.3) | data formatting | bytes 8388608
  915.8 21.2 %psum.7 = f32[2,2,2048]{2,1,0:T(2,128)S(1)} all-reduce(f32[2,2,2048]{2,1,0:T(2,128)S(1)} %pad_maximum_fusion.19), channel_id=1, replica_groups=mesh['dp'=4,'tp'=8] {'tp'}, use_global_device_ids=true, to_apply=%region_52.53 | all-reduce | flops 8192 | bytes 65536 | tf_op jit(solution)/shard_map/psum | solution.py:149
  (539 shorter events, 368.4 us)
Async XLA Ops:
  12.6 76.0 %reduce-scatter.17.cloned.1.call-start = ((), (), s32[]{:S(2)}) async-start(), calls=%async_computation.17 | async-start | bytes 2359296 | tf_op jit(solution)/shard_map/reduce_scatter | solution.py:86
  42.9 78.0 %reduce-scatter.25.cloned.1.call-start = ((), (), s32[]{:S(2)}) async-start(), calls=%async_computation.25 | async-start | bytes 2359296 | tf_op jit(solution)/shard_map/reduce_scatter | solution.py:86
  65.0 81.1 %all-gather.21.cloned.1.call-start = ((), (), s32[]{:S(2)}) async-start(), calls=%async_computation.18 | async-start | bytes 1179648 | tf_op jit(solution)/shard_map/all_gather | solution.py:89
  124.4 73.7 %reduce-scatter.19.cloned.1.call-start = ((), (), s32[]{:S(2)}) async-start(), calls=%async_computation.19 | async-start | bytes 2359296 | tf_op jit(solution)/shard_map/reduce_scatter | solution.py:94
  156.7 74.0 %reduce-scatter.27.cloned.1.call-start = ((), (), s32[]{:S(2)}) async-start(), calls=%async_computation.27 | async-start | bytes 2359296 | tf_op jit(solution)/shard_map/reduce_scatter | solution.py:94
  178.6 78.0 %all-gather.23.cloned.1.call-start = ((), (), s32[]{:S(2)}) async-start(), calls=%async_computation.20 | async-start | bytes 1179648 | tf_op jit(solution)/shard_map/all_gather | solution.py:78
  263.7 72.9 %all-gather.47.cloned.1.call-start = ((), (), s32[]{:S(2)}) async-start(), calls=%async_computation.46 | async-start | bytes 1179648 | tf_op jit(solution)/shard_map/all_gather | solution.py:117
  265.5 92.6 %all-gather.25.cloned.1.call-start = ((), (), s32[]{:S(2)}) async-start(), calls=%async_computation.22 | async-start | bytes 1179648 | tf_op jit(solution)/shard_map/all_gather | solution.py:89
  293.4 94.7 %reduce-scatter.29.cloned.1.call-start = ((), (), s32[]{:S(2)}) async-start(), calls=%async_computation.29 | async-start | bytes 2359296 | tf_op jit(solution)/shard_map/reduce_scatter | solution.py:86
  321.0 99.5 %reduce-scatter.33.cloned.1.call-start = ((), (), s32[]{:S(2)}) async-start(), calls=%async_computation.32 | async-start | bytes 2359296 | tf_op jit(solution)/shard_map/reduce_scatter | solution.py:130
  371.6 72.6 %all-gather.49.cloned.1.call-start = ((), (), s32[]{:S(2)}) async-start(), calls=%async_computation.47 | async-start | bytes 1179648 | tf_op jit(solution)/shard_map/all_gather | solution.py:117
  372.3 93.9 %all-gather.33.cloned.1.call-start = ((), (), s32[]{:S(2)}) async-start(), calls=%async_computation.30 | async-start | bytes 1179648 | tf_op jit(solution)/shard_map/all_gather | solution.py:89
  423.0 84.0 %reduce-scatter.41.cloned.1.call-start = ((), (), s32[]{:S(2)}) async-start(), calls=%async_computation.39 | async-start | bytes 2359296 | tf_op jit(solution)/shard_map/reduce_scatter | solution.py:130
  479.6 59.9 %reduce-scatter.23.cloned.1.call-start = ((), (), s32[]{:S(2)}) async-start(), calls=%async_computation.23 | async-start | bytes 2359296 | tf_op jit(solution)/shard_map/reduce_scatter | solution.py:94
  484.1 87.8 %reduce-scatter.31.cloned.1.call-start = ((), (), s32[]{:S(2)}) async-start(), calls=%async_computation.31 | async-start | bytes 2359296 | tf_op jit(solution)/shard_map/reduce_scatter | solution.py:94
  488.6 108.2 %all-gather.35.cloned.1.call-start = ((), (), s32[]{:S(2)}) async-start(), calls=%async_computation.33 | async-start | bytes 1179648 | tf_op jit(solution)/shard_map/all_gather | solution.py:135
  575.2 73.1 %reduce-scatter.35.cloned.1.call-start = ((), (), s32[]{:S(2)}) async-start(), calls=%async_computation.34 | async-start | bytes 2359296 | tf_op jit(solution)/shard_map/reduce_scatter | solution.py:143
  611.6 69.1 %reduce-scatter.43.cloned.1.call-start = ((), (), s32[]{:S(2)}) async-start(), calls=%async_computation.41 | async-start | bytes 2359296 | tf_op jit(solution)/shard_map/reduce_scatter | solution.py:143
  633.0 75.5 %all-gather.37.cloned.1.call-start = ((), (), s32[]{:S(2)}) async-start(), calls=%async_computation.35 | async-start | bytes 1179648 | tf_op jit(solution)/shard_map/all_gather | solution.py:117
  686.8 73.6 %reduce-scatter.37.cloned.1.call-start = ((), (), s32[]{:S(2)}) async-start(), calls=%async_computation.36 | async-start | bytes 2359296 | tf_op jit(solution)/shard_map/reduce_scatter | solution.py:130
  718.7 74.2 %reduce-scatter.45.cloned.1.call-start = ((), (), s32[]{:S(2)}) async-start(), calls=%async_computation.43 | async-start | bytes 2359296 | tf_op jit(solution)/shard_map/reduce_scatter | solution.py:130
  742.0 77.2 %all-gather.39.cloned.1.call-start = ((), (), s32[]{:S(2)}) async-start(), calls=%async_computation.37 | async-start | bytes 1179648 | tf_op jit(solution)/shard_map/all_gather | solution.py:135
  805.0 109.3 %reduce-scatter.39.cloned.1.call-start = ((), (), s32[]{:S(2)}) async-start(), calls=%async_computation.38 | async-start | bytes 2359296 | tf_op jit(solution)/shard_map/reduce_scatter | solution.py:143
  832.8 81.6 %reduce-scatter.47.cloned.1.call-start = ((), (), s32[]{:S(2)}) async-start(), calls=%async_computation.45 | async-start | bytes 2359296 | tf_op jit(solution)/shard_map/reduce_scatter | solution.py:143
  (166 other events, 1986.7 us)
Sparse Core Ops, SparseCore 0:
  11.9 24.5 all-gather.18
  61.4 27.1 reduce-scatter.16
  91.3 29.6 reduce-scatter.24
  123.8 22.1 all-gather.20
  170.9 27.1 reduce-scatter.18
  200.9 29.6 reduce-scatter.26
  234.4 22.2 all-gather.22
  263.0 27.1 reduce-scatter.20
  292.4 22.2 all-gather.30
  360.9 27.1 reduce-scatter.28
  390.8 29.5 reduce-scatter.32
  421.9 22.2 all-gather.48
  479.8 27.2 reduce-scatter.40
  509.9 29.6 reduce-scatter.22
  542.3 29.6 reduce-scatter.30
  574.5 22.1 all-gather.34
  621.1 27.1 reduce-scatter.34
  651.1 29.6 reduce-scatter.42
  686.2 22.2 all-gather.36
  733.2 27.1 reduce-scatter.36
  763.3 29.6 reduce-scatter.44
  796.9 22.2 all-gather.38
  842.9 27.2 reduce-scatter.38
  872.5 29.4 reduce-scatter.46
  (8 shorter events, 158.1 us)
where the time goes:
time: 958 us; the launch traced here: 947 us
  waiting for transfers between devices  607 us (63%)
  matrix products  196 us (20%)
  other arithmetic  52.4 us (5%)
  local copies, waits for them, and re-layouts  50.4 us (5%)
  blocking collectives  21.2 us (2%)
  between operations  16.4 us (2%)
    reduce_scatter x4, waiting for transfers between devices, device_program(): lax.psum_scatter(down_part, 'tp', scatter_dimension=0, tiled=True)  111 us
    reduce_scatter x4, waiting for transfers between devices, device_program(): lax.psum_scatter(grad_nb_part, 'tp', scatter_dimension=0, tiled=True)  97.4 us
    reduce_scatter x4, waiting for transfers between devices, device_program(): lax.psum_scatter(attn_part, 'tp', scatter_dimension=0, tiled=True)  96.2 us
    all_gather x4, waiting for transfers between devices, device_program(): normed_full = lax.all_gather(normed, 'tp', axis=0, tiled=True)  78.7 us
    all_gather x4, waiting for transfers between devices, device_program(): grad_full = lax.all_gather(grad_in, 'tp', axis=0, tiled=True)  69.6 us
    all_gather x4, waiting for transfers between devices, device_program(): normed_b_full = lax.all_gather(normed_b, 'tp', axis=0, tiled=True)  68.1 us
    reduce_scatter x4, waiting for transfers between devices, device_program(): lax.psum_scatter(grad_n_part, 'tp', scatter_dimension=0, tiled=True)  47.6 us
    unnamed x317, local copies, waits for them, and re-layouts  42.7 us
  transfers between devices with their start and end apart: 32, of which 29 were waited for; matrix products, arithmetic and copies ran while one was open for 25% of the time, Pallas kernels for 0%

commit v1 on v0

v1 whole, which is shorter than its diff:
```python
import functools

import jax
import jax.numpy as jnp
from jax import lax
from jax.experimental import pallas as pl
from jax.experimental.pallas import tpu as pltpu
from jax.sharding import PartitionSpec as P

NORM_EPS = 1e-5
F32 = jnp.float32
BF16 = jnp.bfloat16
MESH = pl.DeviceIdType.MESH
ANY = pl.BlockSpec(memory_space=pl.ANY)
VMEM = pl.BlockSpec(memory_space=pltpu.VMEM)
AG_COPIES = 11
RS_COPIES = 10
NN = (((1,), (0,)), ((), ()))
NT = (((1,), (1,)), ((), ()))
TN = (((0,), (0,)), ((), ()))


def dot(a, b, dims=NN):
    return lax.dot_general(a, b, dims, preferred_element_type=F32)


def aligned(index, size):
    return pl.ds(pl.multiple_of(index * size, size), size)


class Ring:
    def __init__(self, devices, rows, send_sems, recv_sems):
        self.chips = devices // 2
        self.rows = rows
        self.send_sems, self.recv_sems = send_sems, recv_sems
        self.used = 0
        self.me = lax.axis_index('tp')
        self.chip = self.me // 2
        self.core = self.me % 2
        self.right_chip = lax.rem(self.chip + 1, self.chips)
        self.left_chip = lax.rem(self.chip + self.chips - 1, self.chips)
        self.far_chip = lax.rem(self.chip + 2, self.chips)
        self.right = self.right_chip * 2 + self.core
        self.left = self.left_chip * 2 + self.core
        self.far = self.far_chip * 2 + self.core
        self.partner = self.chip * 2 + 1 - self.core
        self.peers = (self.left, self.right, self.partner)

    def greet(self):
        barrier = pltpu.get_barrier_semaphore()
        for peer in self.peers:
            pl.semaphore_signal(barrier, inc=1, device_id={'tp': peer}, device_id_type=MESH)
        pl.semaphore_wait(barrier, len(self.peers))

    def send(self, src, dst, device):
        copy = pltpu.make_async_remote_copy(src, dst, self.send_sems.at[self.used], self.recv_sems.at[self.used],
                                            device_id={'tp': device}, device_id_type=MESH)
        self.used += 1
        copy.start()
        return copy


class Gather:
    def __init__(self, ring, full):
        self.ring, self.full = ring, full
        self.half = ring.rows // 2

    def block(self, owner):
        return self.full.at[aligned(owner, self.ring.rows)]

    def part(self, owner, index):
        return self.full.at[pl.ds(pl.multiple_of(owner * self.ring.rows + index * self.half, self.half), self.half)]

    def start(self):
        ring = self.ring
        low, high, whole = self.part(ring.me, 0), self.part(ring.me, 1), self.block(ring.me)
        self.r0 = ring.send(low, low, ring.right)
        self.l1 = ring.send(high, high, ring.left)
        self.r1 = ring.send(high, high, ring.right)
        self.l0 = ring.send(low, low, ring.left)
        self.own = ring.send(whole, whole, ring.partner)

    def relay(self):
        ring = self.ring
        from_left, from_right = self.part(ring.left, 0), self.part(ring.right, 1)
        self.r0.wait_recv()
        self.relay_r = ring.send(from_left, from_left, ring.right)
        self.l1.wait_recv()
        self.relay_l = ring.send(from_right, from_right, ring.left)
        self.r1.wait_recv()
        left_block = self.block(ring.left)
        self.pass_left = ring.send(left_block, left_block, ring.partner)
        self.l0.wait_recv()
        right_block = self.block(ring.right)
        self.pass_right = ring.send(right_block, right_block, ring.partner)

    def finish(self):
        ring = self.ring
        far_low, far_high = self.part(ring.far, 0), self.part(ring.far, 1)
        self.relay_r.wait_recv()
        self.pass_low = ring.send(far_low, far_low, ring.partner)
        self.relay_l.wait_recv()
        self.pass_high = ring.send(far_high, far_high, ring.partner)
        for copy in (self.own, self.pass_left, self.pass_right, self.pass_low, self.pass_high):
            copy.wait_recv()

    def sent(self):
        for copy in (self.r0, self.l1, self.r1, self.l0, self.own, self.relay_r, self.relay_l, self.pass_left,
                     self.pass_right, self.pass_low, self.pass_high):
            copy.wait_send()


class Reduce:
    def __init__(self, ring, part, bufs):
        self.ring, self.part = ring, part
        self.from_partner, self.sums, self.via_left, self.via_right, self.in_left, self.in_right = bufs
        self.half = ring.rows // 2
        self.chips = (ring.far_chip, ring.right_chip, ring.left_chip, ring.chip)

    def start(self):
        ring = self.ring
        self.swaps = []
        for slot, chip in enumerate(self.chips):
            rows = self.part.at[aligned(chip * 2 + 1 - ring.core, ring.rows)]
            self.swaps.append(ring.send(rows, self.from_partner.at[slot], ring.partner))

    def add(self, slot):
        self.swaps[slot].wait_recv()
        rows = aligned(self.chips[slot] * 2 + self.ring.core, self.ring.rows)
        self.sums[slot] = self.part[rows, :] + self.from_partner[slot]

    def far_out(self):
        ring, half = self.ring, self.half
        self.add(0)
        self.far_r = ring.send(self.sums.at[0, 0:half], self.via_left, ring.right)
        self.far_l = ring.send(self.sums.at[0, half:2 * half], self.via_right, ring.left)

    def near_out(self):
        ring, half = self.ring, self.half
        self.add(1)
        self.near_r = ring.send(self.sums.at[1, half:2 * half], self.in_left.at[half:2 * half], ring.right)
        self.add(2)
        self.near_l = ring.send(self.sums.at[2, 0:half], self.in_right.at[0:half], ring.left)
        self.add(3)

    def relay(self):
        ring, half = self.ring, self.half
        self.far_r.wait_recv()
        self.sums[1, 0:half] = self.sums[1, 0:half] + self.via_left[...]
        self.relay_r = ring.send(self.sums.at[1, 0:half], self.in_left.at[0:half], ring.right)
        self.far_l.wait_recv()
        self.sums[2, half:2 * half] = self.sums[2, half:2 * half] + self.via_right[...]
        self.relay_l = ring.send(self.sums.at[2, half:2 * half], self.in_right.at[half:2 * half], ring.left)

    def finish(self):
        for copy in (self.near_r, self.near_l, self.relay_r, self.relay_l):
            copy.wait_recv()
        return self.sums[3] + self.in_left[...] + self.in_right[...]

    def sent(self):
        for copy in (*self.swaps, self.far_r, self.far_l, self.near_r, self.near_l, self.relay_r, self.relay_l):
            copy.wait_send()


def reduce_scratch(rows, width):
    return [pltpu.VMEM((4, rows, width), F32), pltpu.VMEM((4, rows, width), F32),
            pltpu.VMEM((rows // 2, width), F32), pltpu.VMEM((rows // 2, width), F32),
            pltpu.VMEM((rows, width), F32), pltpu.VMEM((rows, width), F32)]


REDUCE_BUFS = 6


def norm_rows(row_vals, gain_vec):
    vals = row_vals.astype(F32)
    return (vals * lax.rsqrt(jnp.mean(vals * vals, axis=-1, keepdims=True) + NORM_EPS) * gain_vec).astype(BF16)


def norm_rows_backward(row_vals, gain_vec, cot_rows):
    vals = row_vals.astype(F32)
    scale = lax.rsqrt(jnp.mean(vals * vals, axis=-1, keepdims=True) + NORM_EPS)
    unit = vals * scale
    grad_gain = jnp.sum(cot_rows * unit, axis=0, keepdims=True)
    cot_unit = cot_rows * gain_vec
    grad_vals = scale * (cot_unit - unit * jnp.mean(cot_unit * unit, axis=-1, keepdims=True))
    return grad_vals, grad_gain


def head_probs(query, key, score_scale):
    seq_len = query.shape[0]
    scores = dot(query, key, NT) * score_scale
    row_pos = lax.broadcasted_iota(jnp.int32, (seq_len, seq_len), 0)
    col_pos = lax.broadcasted_iota(jnp.int32, (seq_len, seq_len), 1)
    scores = jnp.where(row_pos >= col_pos, scores, -1e30)
    exp_scores = jnp.exp(scores - jnp.max(scores, axis=-1, keepdims=True))
    return exp_scores / jnp.sum(exp_scores, axis=-1, keepdims=True)


def credit_signal(ring, credit):
    for peer in ring.peers:
        pl.semaphore_signal(credit, inc=1, device_id={'tp': peer}, device_id_type=MESH)


def residual(row_vals, total):
    return (row_vals.astype(F32) + total.astype(BF16).astype(F32)).astype(BF16)


def forward_skeleton(ring, rows_ref, gain, out_ref, full, credit, reducers, ready, gathered, partial):
    own = aligned(ring.me, ring.rows)
    ring.greet()
    full[own, :] = norm_rows(rows_ref[0], gain)
    first = Gather(ring, full)
    first.start()
    first.relay()
    first.finish()
    ready()
    gathered(0)
    first.sent()
    credit_signal(ring, credit)
    pl.semaphore_wait(credit, len(ring.peers))
    full[own, :] = norm_rows(rows_ref[1], gain)
    second = Gather(ring, full)
    second.start()
    partial(0)
    reducers[0].start()
    reducers[0].far_out()
    reducers[0].near_out()
    second.relay()
    second.finish()
    gathered(1)
    reducers[0].relay()
    partial(1)
    reducers[1].start()
    reducers[1].far_out()
    reducers[1].near_out()
    out_ref[0] = residual(rows_ref[0], reducers[0].finish())
    reducers[1].relay()
    out_ref[1] = residual(rows_ref[1], reducers[1].finish())
    second.sent()
    reducers[0].sent()
    reducers[1].sent()


def loop_columns(count, body):
    def step(index, carry):
        body(index)
        return carry
    lax.fori_loop(0, count, step, 0)


def attention_forward_kernel(layer, devices, head_dim, groups, rows_ref, gain_ref, w_qkv, w_out, out_ref, qkv_ref, mix_ref,
                             qkv_w, out_w, full, part_a, part_b, *rest):
    bufs_a, bufs_b = rest[:REDUCE_BUFS], rest[REDUCE_BUFS:2 * REDUCE_BUFS]
    load_sem, send_sems, recv_sems, credit = rest[2 * REDUCE_BUFS:]
    ring = Ring(devices, rows_ref.shape[1], send_sems, recv_sems)
    loads = [pltpu.make_async_copy(w_qkv.at[layer], qkv_w, load_sem.at[0]),
             pltpu.make_async_copy(w_out.at[layer], out_w, load_sem.at[1])]
    for load in loads:
        load.start()
    parts = (part_a, part_b)
    reducers = [Reduce(ring, part_a, bufs_a), Reduce(ring, part_b, bufs_b)]

    def ready():
        for load in loads:
            load.wait()

    def gathered(micro):
        qkv_ref[micro] = dot(full[...], qkv_w[...]).astype(BF16)

    def partial(micro):
        key = qkv_ref[micro, :, groups * head_dim:(groups + 1) * head_dim]
        value = qkv_ref[micro, :, (groups + 1) * head_dim:]
        for head in range(groups):
            cols = slice(head * head_dim, (head + 1) * head_dim)
            prob = head_probs(qkv_ref[micro, :, cols], key, head_dim ** -0.5).astype(BF16)
            mix_ref[micro, :, cols] = dot(prob, value).astype(BF16)

        def columns(index):
            cols = aligned(index, 512)
            parts[micro][:, cols] = dot(mix_ref[micro], out_w[:, cols])
        loop_columns(out_w.shape[1] // 512, columns)

    forward_skeleton(ring, rows_ref, gain_ref[layer:layer + 1, :], out_ref, full, credit, reducers, ready, gathered, partial)


def mlp_forward_kernel(layer, devices, rows_ref, gain_ref, w_gate, w_up, w_down, out_ref,
                       gate_w, up_w, down_w, inner, full, part_a, part_b, *rest):
    bufs_a, bufs_b = rest[:REDUCE_BUFS], rest[REDUCE_BUFS:2 * REDUCE_BUFS]
    load_sem, send_sems, recv_sems, credit = rest[2 * REDUCE_BUFS:]
    ring = Ring(devices, rows_ref.shape[1], send_sems, recv_sems)
    loads = [pltpu.make_async_copy(src.at[layer], dst, load_sem.at[index])
             for index, (src, dst) in enumerate(((w_gate, gate_w), (w_up, up_w), (w_down, down_w)))]
    for load in loads:
        load.start()
    parts = (part_a, part_b)
    reducers = [Reduce(ring, part_a, bufs_a), Reduce(ring, part_b, bufs_b)]

    def ready():
        for load in loads:
            load.wait()

    def gathered(micro):
        def columns(index):
            cols = aligned(index, 256)
            gate_pre = dot(full[...], gate_w[:, cols])
            up_proj = dot(full[...], up_w[:, cols])
            inner[:, cols] = (gate_pre * jax.nn.sigmoid(gate_pre) * up_proj).astype(BF16)
        loop_columns(gate_w.shape[1] // 256, columns)

    def partial(micro):
        def columns(index):
            cols = aligned(index, 512)
            parts[micro][:, cols] = dot(inner[...], down_w[:, cols])
        loop_columns(down_w.shape[1] // 512, columns)

    forward_skeleton(ring, rows_ref, gain_ref[layer:layer + 1, :], out_ref, full, credit, reducers, ready, gathered, partial)


def backward_skeleton(ring, rows_ref, cot_ref, gain, out_ref, grad_gain_ref, full, cots, credit, reducers, ready,
                      partial, weights_near, weights_far, weights_out):
    own = aligned(ring.me, ring.rows)
    ring.greet()
    full[own, :] = norm_rows(rows_ref[0], gain)
    first = Gather(ring, full)
    first.start()
    for micro in range(2):
        cots[micro, own, :] = cot_ref[micro]
    cot_gathers = [Gather(ring, cots.at[micro]) for micro in range(2)]
    cot_gathers[0].start()
    first.relay()
    first.finish()
    cot_gathers[0].relay()
    cot_gathers[1].start()
    cot_gathers[0].finish()
    ready()
    partial(0)
    reducers[0].start()
    reducers[0].far_out()
    reducers[0].near_out()
    weights_near(0)
    first.sent()
    credit_signal(ring, credit)
    cot_gathers[1].relay()
    reducers[0].relay()
    cot_gathers[1].finish()
    pl.semaphore_wait(credit, len(ring.peers))
    full[own, :] = norm_rows(rows_ref[1], gain)
    second = Gather(ring, full)
    second.start()
    weights_far(0)
    second.relay()
    second.finish()
    partial(1)
    reducers[1].start()
    reducers[1].far_out()
    reducers[1].near_out()
    total = reducers[0].finish().astype(BF16).astype(F32)
    grad_rows, grad_gain_0 = norm_rows_backward(rows_ref[0], gain, total)
    out_ref[0] = (cot_ref[0].astype(F32) + grad_rows).astype(BF16)
    weights_near(1)
    reducers[1].relay()
    weights_far(1)
    weights_out()
    total = reducers[1].finish().astype(BF16).astype(F32)
    grad_rows, grad_gain_1 = norm_rows_backward(rows_ref[1], gain, total)
    out_ref[1] = (cot_ref[1].astype(F32) + grad_rows).astype(BF16)
    grad_gain_ref[...] = grad_gain_0 + grad_gain_1
    second.sent()
    for micro in range(2):
        cot_gathers[micro].sent()
        reducers[micro].sent()


def mlp_backward_kernel(layer, devices, rows_ref, cot_ref, gain_ref, w_gate, w_up, w_down,
                        out_ref, grad_gain_ref, grad_gate_out, grad_up_out, grad_down_out,
                        gate_w, up_w, down_w, inner, grad_gate, grad_up, acc_gate, acc_up, acc_down,
                        stage_gate, stage_up, stage_down, full, cots, part_a, part_b, *rest):
    bufs_a, bufs_b = rest[:REDUCE_BUFS], rest[REDUCE_BUFS:2 * REDUCE_BUFS]
    load_sem, store_sem, send_sems, recv_sems, credit = rest[2 * REDUCE_BUFS:]
    ring = Ring(devices, rows_ref.shape[1], send_sems, recv_sems)
    loads = [pltpu.make_async_copy(src.at[layer], dst, load_sem.at[index])
             for index, (src, dst) in enumerate(((w_gate, gate_w), (w_up, up_w), (w_down, down_w)))]
    for load in loads:
        load.start()
    parts = (part_a, part_b)
    reducers = [Reduce(ring, part_a, bufs_a), Reduce(ring, part_b, bufs_b)]
    stores = [pltpu.make_async_copy(src, dst, store_sem.at[index]) for index, (src, dst) in enumerate(
        ((stage_gate, grad_gate_out), (stage_up, grad_up_out), (stage_down, grad_down_out)))]

    def ready():
        for load in loads:
            load.wait()

    def partial(micro):
        def columns(index):
            cols = aligned(index, 256)
            gate_pre = dot(full[...], gate_w[:, cols])
            up_proj = dot(full[...], up_w[:, cols])
            grad_inner = dot(cots[micro], down_w[cols, :], NT).astype(BF16).astype(F32)
            gate_sig = jax.nn.sigmoid(gate_pre)
            gate_act = gate_pre * gate_sig
            inner[:, cols] = (gate_act * up_proj).astype(BF16)
            grad_up[:, cols] = (grad_inner * gate_act).astype(BF16)
            grad_gate[:, cols] = (grad_inner * up_proj * gate_sig * (1.0 + gate_pre * (1.0 - gate_sig))).astype(BF16)
        loop_columns(gate_w.shape[1] // 256, columns)

        def out_columns(index):
            cols = aligned(index, 256)
            parts[micro][:, cols] = dot(grad_gate[...], gate_w[cols, :], NT) + dot(grad_up[...], up_w[cols, :], NT)
        loop_columns(gate_w.shape[0] // 256, out_columns)

    def put(micro, acc, stage, rows, term):
        if micro == 0:
            acc[rows, :] = term
        else:
            stage[rows, :] = (acc[rows, :] + term).astype(BF16)

    def weights_near(micro):
        def columns(index):
            cols = aligned(index, 256)
            put(micro, acc_gate, stage_gate, cols, dot(full[:, cols], grad_gate[...], TN))
            put(micro, acc_up, stage_up, cols, dot(full[:, cols], grad_up[...], TN))
        loop_columns(full.shape[1] // 256, columns)
        if micro == 1:
            stores[0].start()
            stores[1].start()

    def weights_far(micro):
        def columns(index):
            cols = aligned(index, 128)
            put(micro, acc_down, stage_down, cols, dot(inner[:, cols], cots[micro], TN))
        loop_columns(inner.shape[1] // 128, columns)
        if micro == 1:
            stores[2].start()

    def weights_out():
        for store in stores:
            store.wait()

    backward_skeleton(ring, rows_ref, cot_ref, gain_ref[layer:layer + 1, :], out_ref, grad_gain_ref, full, cots, credit,
                      reducers, ready, partial, weights_near, weights_far, weights_out)


def attention_backward_kernel(layer, devices, head_dim, groups, rows_ref, cot_ref, gain_ref, qkv_ref, mix_ref, w_qkv, w_out,
                              out_ref, grad_gain_ref, grad_qkv_out, grad_out_out,
                              qkv_w, out_w, grad_mix, grad_qkv, acc_qkv, acc_out, stage_qkv, stage_out,
                              full, cots, part_a, part_b, *rest):
    bufs_a, bufs_b = rest[:REDUCE_BUFS], rest[REDUCE_BUFS:2 * REDUCE_BUFS]
    load_sem, store_sem, send_sems, recv_sems, credit = rest[2 * REDUCE_BUFS:]
    ring = Ring(devices, rows_ref.shape[1], send_sems, recv_sems)
    loads = [pltpu.make_async_copy(w_qkv.at[layer], qkv_w, load_sem.at[0]),
             pltpu.make_async_copy(w_out.at[layer], out_w, load_sem.at[1])]
    for load in loads:
        load.start()
    parts = (part_a, part_b)
    reducers = [Reduce(ring, part_a, bufs_a), Reduce(ring, part_b, bufs_b)]
    stores = [pltpu.make_async_copy(stage_qkv, grad_qkv_out, store_sem.at[0]),
              pltpu.make_async_copy(stage_out, grad_out_out, store_sem.at[1])]

    def ready():
        for load in loads:
            load.wait()

    def partial(micro):
        grad_mix[...] = dot(cots[micro], out_w[...], NT).astype(BF16)
        score_scale = head_dim ** -0.5
        key = qkv_ref[micro, :, groups * head_dim:(groups + 1) * head_dim]
        value = qkv_ref[micro, :, (groups + 1) * head_dim:]
        grad_key = grad_value = None
        for head in range(groups):
            cols = slice(head * head_dim, (head + 1) * head_dim)
            query = qkv_ref[micro, :, cols]
            head_grad = grad_mix[:, cols]
            prob = head_probs(query, key, score_scale)
            grad_prob = dot(head_grad, value, NT).astype(BF16).astype(F32)
            row_dot = jnp.sum(grad_prob * prob, axis=-1, keepdims=True)
            grad_scores = (prob * (grad_prob - row_dot) * score_scale).astype(BF16)
            grad_qkv[:, cols] = dot(grad_scores, key).astype(BF16)
            key_term = dot(grad_scores, query, TN)
            value_term = dot(prob.astype(BF16), head_grad, TN)
            grad_key = key_term if grad_key is None else grad_key + key_term
            grad_value = value_term if grad_value is None else grad_value + value_term
        grad_qkv[:, groups * head_dim:(groups + 1) * head_dim] = grad_key.astype(BF16)
        grad_qkv[:, (groups + 1) * head_dim:] = grad_value.astype(BF16)

        def columns(index):
            cols = aligned(index, 256)
            parts[micro][:, cols] = dot(grad_qkv[...], qkv_w[cols, :], NT)
        loop_columns(qkv_w.shape[0] // 256, columns)

    def put(micro, acc, stage, rows, term):
        if micro == 0:
            acc[rows, :] = term
        else:
            stage[rows, :] = (acc[rows, :] + term).astype(BF16)

    def weights_near(micro):
        def columns(index):
            cols = aligned(index, 256)
            put(micro, acc_qkv, stage_qkv, cols, dot(full[:, cols], grad_qkv[...], TN))
        loop_columns(full.shape[1] // 256, columns)
        if micro == 1:
            stores[0].start()

    def weights_far(micro):
        def columns(index):
            cols = aligned(index, 128)
            put(micro, acc_out, stage_out, cols, dot(mix_ref[micro, :, cols], cots[micro], TN))
        loop_columns(mix_ref.shape[2] // 128, columns)
        if micro == 1:
            stores[1].start()

    def weights_out():
        for store in stores:
            store.wait()

    backward_skeleton(ring, rows_ref, cot_ref, gain_ref[layer:layer + 1, :], out_ref, grad_gain_ref, full, cots, credit,
                      reducers, ready, partial, weights_near, weights_far, weights_out)


def gain_sum_kernel(devices, part_ref, out_ref, held, send_sems, recv_sems):
    me = lax.axis_index('tp')
    barrier = pltpu.get_barrier_semaphore()
    others = [lax.rem(me + step, devices) for step in range(1, devices)]
    for peer in others:
        pl.semaphore_signal(barrier, inc=1, device_id={'tp': peer}, device_id_type=MESH)
    pl.semaphore_wait(barrier, len(others))
    copies = []
    for index, peer in enumerate(others):
        copy = pltpu.make_async_remote_copy(part_ref, held.at[me], send_sems.at[index], recv_sems.at[index],
                                            device_id={'tp': peer}, device_id_type=MESH)
        copy.start()
        copies.append(copy)
    held[me] = part_ref[...]
    for copy in copies:
        copy.wait()
    total = held[0]
    for index in range(1, devices):
        total = total + held[index]
    out_ref[...] = total


def comm_params(collective_id):
    return pltpu.CompilerParams(collective_id=collective_id, has_side_effects=True, vmem_limit_bytes=64_000_000)


def solution(mesh):
    devices = mesh.shape['tp']
    row_spec = P(None, ('dp', 'tp'), None)
    gain_spec = P(None, None)
    qkv_spec = P(None, None, 'tp', None, None)
    head_spec = P(None, 'tp', None, None)
    col_spec = P(None, None, 'tp')
    row_shard_spec = P(None, 'tp', None)

    def device_program(x_in, y_cot, gain_attn, gain_mlp, w_qkv, w_out, w_gate, w_up, w_down):
        micro_count, rows, width = x_in.shape
        layer_count = w_qkv.shape[0]
        groups = w_qkv.shape[3] - 2
        head_dim = w_qkv.shape[4]
        seq_len = rows * devices
        qkv_width = (groups + 2) * head_dim
        mix_width = groups * head_dim
        inner_width = w_gate.shape[2]
        w_qkv_flat = w_qkv.reshape(layer_count, width, qkv_width)
        w_out_flat = w_out.reshape(layer_count, mix_width, width)
        row_shape = jax.ShapeDtypeStruct(x_in.shape, BF16)
        gain_shape = jax.ShapeDtypeStruct((1, width), F32)

        def bf16(*shape):
            return pltpu.VMEM(shape, BF16)

        def f32(*shape):
            return pltpu.VMEM(shape, F32)

        def sems(gathers):
            count = gathers * AG_COPIES + 2 * RS_COPIES
            return [pltpu.SemaphoreType.DMA((count,)), pltpu.SemaphoreType.DMA((count,)), pltpu.SemaphoreType.REGULAR]

        full = bf16(seq_len, width)
        reduce_bufs = [f32(seq_len, width), f32(seq_len, width)] + reduce_scratch(rows, width) + reduce_scratch(rows, width)
        attn_weights = [bf16(width, qkv_width), bf16(mix_width, width)]
        mlp_weights = [bf16(width, inner_width), bf16(width, inner_width), bf16(inner_width, width)]

        layer_rows, hidden_rows, qkv_kept, mix_kept = [], [], [], []
        layer_in = x_in
        for layer in range(layer_count):
            layer_rows.append(layer_in)
            hidden, qkv_heads, mix = pl.pallas_call(
                functools.partial(attention_forward_kernel, layer, devices, head_dim, groups),
                out_shape=(row_shape, jax.ShapeDtypeStruct((micro_count, seq_len, qkv_width), BF16),
                           jax.ShapeDtypeStruct((micro_count, seq_len, mix_width), BF16)),
                in_specs=[VMEM, VMEM, ANY, ANY], out_specs=(VMEM, VMEM, VMEM),
                scratch_shapes=attn_weights + [full] + reduce_bufs + [pltpu.SemaphoreType.DMA((2,))] + sems(2),
                compiler_params=comm_params(4 * layer), name=f'attn_fwd_{layer}',
            )(layer_in, gain_attn, w_qkv_flat, w_out_flat)
            qkv_kept.append(qkv_heads)
            mix_kept.append(mix)
            hidden_rows.append(hidden)
            layer_in = pl.pallas_call(
                functools.partial(mlp_forward_kernel, layer, devices),
                out_shape=row_shape, in_specs=[VMEM, VMEM, ANY, ANY, ANY], out_specs=VMEM,
                scratch_shapes=mlp_weights + [bf16(seq_len, inner_width), full] + reduce_bufs
                + [pltpu.SemaphoreType.DMA((3,))] + sems(2),
                compiler_params=comm_params(4 * layer + 1), name=f'mlp_fwd_{layer}',
            )(hidden, gain_mlp, w_gate, w_up, w_down)
        y_rows = layer_in

        grads = [[None] * layer_count for unused in range(5)]
        gain_a, gain_b = [None] * layer_count, [None] * layer_count
        cots = bf16(2, seq_len, width)
        grad_in = y_cot
        for layer in reversed(range(layer_count)):
            grad_hidden, gain_b[layer], grads[2][layer], grads[3][layer], grads[4][layer] = pl.pallas_call(
                functools.partial(mlp_backward_kernel, layer, devices),
                out_shape=(row_shape, gain_shape, jax.ShapeDtypeStruct((width, inner_width), BF16),
                           jax.ShapeDtypeStruct((width, inner_width), BF16), jax.ShapeDtypeStruct((inner_width, width), BF16)),
                in_specs=[VMEM, VMEM, VMEM, ANY, ANY, ANY], out_specs=(VMEM, VMEM, ANY, ANY, ANY),
                scratch_shapes=mlp_weights + [bf16(seq_len, inner_width)] * 3
                + [f32(width, inner_width), f32(width, inner_width), f32(inner_width, width)]
                + mlp_weights + [full, cots] + reduce_bufs
                + [pltpu.SemaphoreType.DMA((3,)), pltpu.SemaphoreType.DMA((3,))] + sems(4),
                compiler_params=comm_params(4 * layer + 2), name=f'mlp_bwd_{layer}',
            )(hidden_rows[layer], grad_in, gain_mlp, w_gate, w_up, w_down)
            grad_in, gain_a[layer], grads[0][layer], grads[1][layer] = pl.pallas_call(
                functools.partial(attention_backward_kernel, layer, devices, head_dim, groups),
                out_shape=(row_shape, gain_shape, jax.ShapeDtypeStruct((width, qkv_width), BF16),
                           jax.ShapeDtypeStruct((mix_width, width), BF16)),
                in_specs=[VMEM, VMEM, VMEM, VMEM, VMEM, ANY, ANY], out_specs=(VMEM, VMEM, ANY, ANY),
                scratch_shapes=attn_weights + [bf16(seq_len, mix_width), bf16(seq_len, qkv_width)]
                + [f32(width, qkv_width), f32(mix_width, width)] + attn_weights + [full, cots] + reduce_bufs
                + [pltpu.SemaphoreType.DMA((2,)), pltpu.SemaphoreType.DMA((2,))] + sems(4),
                compiler_params=comm_params(4 * layer + 3), name=f'attn_bwd_{layer}',
            )(layer_rows[layer], grad_hidden, gain_attn, qkv_kept[layer], mix_kept[layer], w_qkv_flat, w_out_flat)

        gain_part = jnp.concatenate(gain_a + gain_b, axis=0)
        gain_sum = pl.pallas_call(
            functools.partial(gain_sum_kernel, devices),
            out_shape=jax.ShapeDtypeStruct(gain_part.shape, F32), in_specs=[VMEM], out_specs=VMEM,
            scratch_shapes=[pltpu.VMEM((devices, *gain_part.shape), F32), pltpu.SemaphoreType.DMA((devices - 1,)),
                            pltpu.SemaphoreType.DMA((devices - 1,))],
            compiler_params=comm_params(4 * layer_count), name='gain_sum',
        )(gain_part)
        return (y_rows, grad_in,
                jnp.stack(grads[0]).reshape(w_qkv.shape), jnp.stack(grads[1]).reshape(w_out.shape),
                jnp.stack(grads[2]), jnp.stack(grads[3]), jnp.stack(grads[4]),
                gain_sum[:layer_count], gain_sum[layer_count:])

    return jax.shard_map(device_program, mesh=mesh,
                         in_specs=(row_spec, row_spec, gain_spec, gain_spec, qkv_spec, head_spec, col_spec, col_spec, row_shard_spec),
                         out_specs=(row_spec, row_spec, P('dp', None, 'tp', None, None), P('dp', 'tp', None, None), P('dp', None, 'tp'), P('dp', None, 'tp'), P('dp', 'tp', None), P('dp', None), P('dp', None)),
                         check_vma=False)
```

time: 958 us -> 491 us (0.51)
  waiting for transfers between devices: 607 us -> 0 us
  Pallas kernels: 0 us -> 440 us
  matrix products: 196 us -> 0 us
  local copies, waits for them, and re-layouts: 50.4 us -> 16.6 us
  other arithmetic: 52.4 us -> 23.5 us
  blocking collectives: 21.2 us -> 0 us
  between operations: 16.4 us -> 1.23 us
    pallas_call x0 -> x9, Pallas kernels: none -> 440 us  [the longest x2 129 us: device_program(): pl.pallas_call(functools.partial(mlp_backward_kernel, layer, devices), ou...]
    reduce_scatter x16 -> x0, waiting for transfers between devices: 352 us -> none  [the longest x4 111 us: device_program(): lax.psum_scatter(down_part, 'tp', scatter_dimension=0, tiled=True)]
    all_gather x16 -> x0, waiting for transfers between devices: 249 us -> none  [the longest x4 78.7 us: device_program(): normed_full = lax.all_gather(normed, 'tp', axis=0, tiled=True)]
    dot_general x84 -> x0, matrix products: 196 us -> none  [the longest x4 16 us: device_program(): jnp.einsum('sd,fd->sf', grad_full, w_down[layer_idx], preferred_element_t...]
    unnamed x317 -> x18, local copies, waits for them, and re-layouts: 42.7 us -> 1.44 us
    psum x1 -> x0, blocking collectives: 21.2 us -> none  [device_program(): lax.psum(jnp.stack([jnp.stack(gain_a_acc), jnp.stack(gain_b_acc)]), 'tp')]
    reduce_sum x15 -> x0, other arithmetic: 17.8 us -> none  [the longest x5 9.3 us: rms_scale(): row_vals * lax.rsqrt(jnp.mean(row_vals * row_vals, axis=-1, keepdims=True...]
    convert_element_type x7 -> x0, other arithmetic: 11.6 us -> none  [the longest x4 5.11 us: norm_apply(): rms_scale(row_vals.astype(jnp.float32), gain_vec).astype(jnp.bfloat16)]
  transfers between devices with their start and end apart: 32 -> 0, of which waited for: 29 -> 0; matrix products, arithmetic and copies ran while one was open for 25% -> 0% of each run, Pallas kernels for 0% -> 0%
where the time goes in v1:
time: 491 us; the launch traced here: 481 us
  Pallas kernels  440 us (90%)
  other arithmetic  23.5 us (5%)
  local copies, waits for them, and re-layouts  16.6 us (3%)
    pallas_call x2, Pallas kernels, device_program(): pl.pallas_call(functools.partial(mlp_backward_kernel, layer, devices), ou...  129 us
    pallas_call x2, Pallas kernels, device_program(): pl.pallas_call(functools.partial(attention_backward_kernel, layer, device...  119 us
    pallas_call x2, Pallas kernels, device_program(): pl.pallas_call(functools.partial(mlp_forward_kernel, layer, devices), out...  93 us
    pallas_call x2, Pallas kernels, device_program(): pl.pallas_call(functools.partial(attention_forward_kernel, layer, devices...  88.4 us
    another operation x1, other arithmetic, device_program(): jnp.stack(grads[2])  10.4 us
    pallas_call x1, Pallas kernels, device_program(): pl.pallas_call(functools.partial(gain_sum_kernel, devices), out_shape=jax...  10.1 us

profile of v1, /device:TPU:81, one launch (start us, length us, event | category | flops | bytes accessed | tf_op | source)
XLA Modules:
  0.0 481.4 jit_solution(16523943317664556268)
XLA Ops:
  0.6 7.2 %reshape.34.w_qkv = bf16[2,2048,512]{2,1,0:T(8,128)(2,1)} reshape(bf16[2,2048,1,4,128]{4,3,2,1,0:T(4,128)(2,1)} %param.13) | data formatting | bytes 8388608 | tf_op jit(solution)/shard_map/reshape | solution.py:565
  7.8 44.5 %attn_fwd_0.1 = (bf16[2,32,2048]{2,1,0:T(8,128)(2,1)}, bf16[2,256,512]{2,1,0:T(8,128)(2,1)}, bf16[2,256,256]{2,1,0:T(8,128)(2,1)}) custom-call(bf16[2,32,2048]{2,1,0:T(8,128)(2,1)} %rows_ref.3, f32[2,2048]{1,0:T(2,128)} %gain_ref.15, bf16[2,2048,512]{2,1,0:T(8,128)(2,1)} %reshape.34.w_qkv, bf16[2,256,2048]{2,1,0:T(8,128)(2,1)} %bitcast.11), custom_call_target="tpu_custom_call" | custom-call | tf_op jit(solution)/shard_map/attn_fwd_0/pallas_call | solution.py:589
  52.3 46.4 %mlp_fwd_0.1.rows_ref = bf16[2,32,2048]{2,1,0:T(8,128)(2,1)} custom-call(bf16[2,32,2048]{2,1,0:T(8,128)(2,1)} %get-tuple-element.33.rows_ref, f32[2,2048]{1,0:T(2,128)} %gain_ref.14, bf16[2,2048,768]{2,1,0:T(8,128)(2,1)} %w_gate.7, bf16[2,2048,768]{2,1,0:T(8,128)(2,1)} %w_up.7, bf16[2,768,2048]{2,1,0:T(8,128)(2,1)} %w_down.7), custom_call_target="tpu_custom_call" | custom-call | tf_op jit(solution)/shard_map/mlp_fwd_0/pallas_call | solution.py:600
  98.7 44.0 %attn_fwd_1.1 = (bf16[2,32,2048]{2,1,0:T(8,128)(2,1)}, bf16[2,256,512]{2,1,0:T(8,128)(2,1)}, bf16[2,256,256]{2,1,0:T(8,128)(2,1)}) custom-call(bf16[2,32,2048]{2,1,0:T(8,128)(2,1)} %mlp_fwd_0.1.rows_ref, f32[2,2048]{1,0:T(2,128)} %gain_ref.15, bf16[2,2048,512]{2,1,0:T(8,128)(2,1)} %reshape.34.w_qkv, bf16[2,256,2048]{2,1,0:T(8,128)(2,1)} %bitcast.12), custom_call_target="tpu_custom_call" | custom-call | tf_op jit(solution)/shard_map/attn_fwd_1/pallas_call | solution.py:589
  142.7 46.6 %mlp_fwd_1.1 = bf16[2,32,2048]{2,1,0:T(8,128)(2,1)} custom-call(bf16[2,32,2048]{2,1,0:T(8,128)(2,1)} %get-tuple-element.34.rows_ref, f32[2,2048]{1,0:T(2,128)} %gain_ref.14, bf16[2,2048,768]{2,1,0:T(8,128)(2,1)} %w_gate.7, bf16[2,2048,768]{2,1,0:T(8,128)(2,1)} %w_up.7, bf16[2,768,2048]{2,1,0:T(8,128)(2,1)} %w_down.7), custom_call_target="tpu_custom_call" | custom-call | tf_op jit(solution)/shard_map/mlp_fwd_1/pallas_call | solution.py:600
  189.3 64.5 %mlp_bwd_1.1 = (bf16[2,32,2048]{2,1,0:T(8,128)(2,1)}, f32[1,2048]{1,0:T(1,128)}, bf16[2048,768]{1,0:T(8,128)(2,1)}, bf16[2048,768]{1,0:T(8,128)(2,1)}, bf16[768,2048]{1,0:T(8,128)(2,1)}) custom-call(bf16[2,32,2048]{2,1,0:T(8,128)(2,1)} %get-tuple-element.34.rows_ref, bf16[2,32,2048]{2,1,0:T(8,128)(2,1)} %cot_ref.1, f32[2,2048]{1,0:T(2,128)} %gain_ref.14, ...), custom_call_target="tpu_custom_call" | custom-call | tf_op jit(solution)/shard_map/mlp_bwd_1/pallas_call | solution.py:614
  253.8 59.6 %attn_bwd_1.1 = (bf16[2,32,2048]{2,1,0:T(8,128)(2,1)}, f32[1,2048]{1,0:T(1,128)}, bf16[2048,512]{1,0:T(8,128)(2,1)}, bf16[256,2048]{1,0:T(8,128)(2,1)}) custom-call(bf16[2,32,2048]{2,1,0:T(8,128)(2,1)} %mlp_fwd_0.1.rows_ref, bf16[2,32,2048]{2,1,0:T(8,128)(2,1)} %get-tuple-element.35.cot_ref, f32[2,2048]{1,0:T(2,128)} %gain_ref.15, ...), custom_call_target="tpu_custom_call" | custom-call | tf_op jit(solution)/shard_map/attn_bwd_1/pallas_call | solution.py:625
  313.4 2.6 stack.46
  315.9 64.9 %mlp_bwd_0.1 = (bf16[2,32,2048]{2,1,0:T(8,128)(2,1)}, f32[1,2048]{1,0:T(1,128)}, bf16[2048,768]{1,0:T(8,128)(2,1)}, bf16[2048,768]{1,0:T(8,128)(2,1)}, bf16[768,2048]{1,0:T(8,128)(2,1)}) custom-call(bf16[2,32,2048]{2,1,0:T(8,128)(2,1)} %get-tuple-element.33.rows_ref, bf16[2,32,2048]{2,1,0:T(8,128)(2,1)} %get-tuple-element.38.cot_ref, f32[2,2048]{1,0:T(2,128)} %gain_ref.14, ...), custom_call_target="tpu_custom_call" | custom-call | tf_op jit(solution)/shard_map/mlp_bwd_0/pallas_call | solution.py:614
  380.9 59.6 %attn_bwd_0.1 = (bf16[2,32,2048]{2,1,0:T(8,128)(2,1)}, f32[1,2048]{1,0:T(1,128)}, bf16[2048,512]{1,0:T(8,128)(2,1)}, bf16[256,2048]{1,0:T(8,128)(2,1)}) custom-call(bf16[2,32,2048]{2,1,0:T(8,128)(2,1)} %rows_ref.3, bf16[2,32,2048]{2,1,0:T(8,128)(2,1)} %get-tuple-element.39.cot_ref, f32[2,2048]{1,0:T(2,128)} %gain_ref.15, ...), custom_call_target="tpu_custom_call" | custom-call | tf_op jit(solution)/shard_map/attn_bwd_0/pallas_call | solution.py:625
  440.5 0.0 copy-start.4
  440.5 0.0 copy-start.5
  440.5 0.0 copy-start.6
  440.5 10.4 %pad_maximum_fusion = (bf16[2,2048,768]{2,1,0:T(8,128)(2,1)}, bf16[2,2048,768]{2,1,0:T(8,128)(2,1)}) fusion(bf16[1,2048,768]{2,1,0:T(8,128)(2,1)} %bitcast.17, bf16[1,2048,768]{2,1,0:T(8,128)(2,1)} %bitcast.19, bf16[1,2048,768]{2,1,0:T(8,128)(2,1)} %bitcast.18, bf16[1,2048,768]{2,1,0:T(8,128)(2,1)} %bitcast.20), kind=kLoop, calls=%fused_computation | loop fusion | flops 6291456 | bytes 25165824 | tf_op jit(solution)/shard_map/stack | solution.py:646
  450.9 0.0 copy-done.4
  450.9 0.7 pad_maximum_fusion.5.part_ref
  451.6 10.1 %gain_sum.1 = f32[4,2048]{1,0:T(4,128)} custom-call(f32[4,2048]{1,0:T(4,128)} %pad_maximum_fusion.5.part_ref), custom_call_target="tpu_custom_call" | custom-call | tf_op jit(solution)/shard_map/gain_sum/pallas_call | solution.py:637
  461.7 1.5 fusion
  463.1 3.1 pad_maximum_fusion.4
  466.2 4.0 stack.45
  470.1 6.1 %pad_maximum_fusion.3 = bf16[2,2048,1,4,128]{4,3,2,1,0:T(4,128)(2,1)} fusion(bf16[1,2048,1,4,128]{4,3,2,1,0:T(4,128)(2,1)S(1)} %bitcast.15, bf16[1,2048,1,4,128]{4,3,2,1,0:T(4,128)(2,1)} %bitcast.16), kind=kLoop, calls=%fused_computation.3 | loop fusion | flops 2097152 | bytes 8388608 | tf_op jit(solution)/shard_map/stack | solution.py:645
  476.3 3.2 pad_maximum_fusion.2
  479.5 0.7 copy.22
  480.2 0.7 copy.23
  (12 shorter events, 0.0 us)
Async XLA Ops:
  440.5 10.4 %copy-start.4 = (f32[1,2048]{1,0:T(1,128)S(1)}, f32[1,2048]{1,0:T(1,128)}, u32[]{:S(2)}) copy-start(f32[1,2048]{1,0:T(1,128)} %get-tuple-element.56) | copy-start | bytes 24580
  440.5 10.4 %copy-start.5 = (f32[1,2048]{1,0:T(1,128)S(1)}, f32[1,2048]{1,0:T(1,128)}, u32[]{:S(2)}) copy-start(f32[1,2048]{1,0:T(1,128)} %get-tuple-element.54) | copy-start | bytes 24580
  440.5 10.4 %copy-start.6 = (f32[1,2048]{1,0:T(1,128)S(1)}, f32[1,2048]{1,0:T(1,128)}, u32[]{:S(2)}) copy-start(f32[1,2048]{1,0:T(1,128)} %get-tuple-element.55) | copy-start | bytes 24580
  440.5 10.4 %copy-start.7 = (f32[1,2048]{1,0:T(1,128)S(1)}, f32[1,2048]{1,0:T(1,128)}, u32[]{:S(2)}) copy-start(f32[1,2048]{1,0:T(1,128)} %get-tuple-element.53) | copy-start | bytes 24580
  470.1 6.1 %copy-start = (bf16[768,2048]{1,0:T(8,128)(2,1)S(1)}, bf16[768,2048]{1,0:T(8,128)(2,1)}, u32[]{:S(2)}) copy-start(bf16[768,2048]{1,0:T(8,128)(2,1)} %get-tuple-element.52) | copy-start | bytes 9437188
  470.1 6.1 %copy-start.1 = (bf16[768,2048]{1,0:T(8,128)(2,1)S(1)}, bf16[768,2048]{1,0:T(8,128)(2,1)}, u32[]{:S(2)}) copy-start(bf16[768,2048]{1,0:T(8,128)(2,1)} %get-tuple-element.51) | copy-start | bytes 9437188
  476.3 3.3 copy-start.2
  476.3 4.0 copy-start.3

commit v2 on v0

v2 whole, which is shorter than its diff:
```python
import functools

import jax
import jax.numpy as jnp
from jax import lax
from jax.experimental import pallas as pl
from jax.experimental.pallas import tpu as pltpu
from jax.sharding import PartitionSpec as P

NORM_EPS = 1e-5
F32 = jnp.float32
BF16 = jnp.bfloat16
MESH = pl.DeviceIdType.MESH
ANY = pl.BlockSpec(memory_space=pl.ANY)
VMEM = pl.BlockSpec(memory_space=pltpu.VMEM)
AG_COPIES = 11
RS_COPIES = 10
NN = (((1,), (0,)), ((), ()))
NT = (((1,), (1,)), ((), ()))
TN = (((0,), (0,)), ((), ()))


def dot(a, b, dims=NN):
    return lax.dot_general(a, b, dims, preferred_element_type=F32)


def aligned(index, size):
    return pl.ds(pl.multiple_of(index * size, size), size)


class Ring:
    def __init__(self, devices, rows, send_sems, recv_sems):
        self.chips = devices // 2
        self.rows = rows
        self.send_sems, self.recv_sems = send_sems, recv_sems
        self.used = 0
        self.me = lax.axis_index('tp')
        self.chip = self.me // 2
        self.core = self.me % 2
        self.right_chip = lax.rem(self.chip + 1, self.chips)
        self.left_chip = lax.rem(self.chip + self.chips - 1, self.chips)
        self.far_chip = lax.rem(self.chip + 2, self.chips)
        self.right = self.right_chip * 2 + self.core
        self.left = self.left_chip * 2 + self.core
        self.far = self.far_chip * 2 + self.core
        self.partner = self.chip * 2 + 1 - self.core
        self.peers = (self.left, self.right, self.partner)

    def greet(self):
        barrier = pltpu.get_barrier_semaphore()
        for peer in self.peers:
            pl.semaphore_signal(barrier, inc=1, device_id={'tp': peer}, device_id_type=MESH)
        pl.semaphore_wait(barrier, len(self.peers))

    def send(self, src, dst, device):
        copy = pltpu.make_async_remote_copy(src, dst, self.send_sems.at[self.used], self.recv_sems.at[self.used],
                                            device_id={'tp': device}, device_id_type=MESH)
        self.used += 1
        copy.start()
        return copy


class Gather:
    def __init__(self, ring, full):
        self.ring, self.full = ring, full
        self.half = ring.rows // 2

    def block(self, owner):
        return self.full.at[aligned(owner, self.ring.rows)]

    def part(self, owner, index):
        return self.full.at[pl.ds(pl.multiple_of(owner * self.ring.rows + index * self.half, self.half), self.half)]

    def start(self):
        ring = self.ring
        low, high, whole = self.part(ring.me, 0), self.part(ring.me, 1), self.block(ring.me)
        self.r0 = ring.send(low, low, ring.right)
        self.l1 = ring.send(high, high, ring.left)
        self.r1 = ring.send(high, high, ring.right)
        self.l0 = ring.send(low, low, ring.left)
        self.own = ring.send(whole, whole, ring.partner)

    def relay(self):
        ring = self.ring
        from_left, from_right = self.part(ring.left, 0), self.part(ring.right, 1)
        self.r0.wait_recv()
        self.relay_r = ring.send(from_left, from_left, ring.right)
        self.l1.wait_recv()
        self.relay_l = ring.send(from_right, from_right, ring.left)
        self.r1.wait_recv()
        left_block = self.block(ring.left)
        self.pass_left = ring.send(left_block, left_block, ring.partner)
        self.l0.wait_recv()
        right_block = self.block(ring.right)
        self.pass_right = ring.send(right_block, right_block, ring.partner)

    def finish(self):
        ring = self.ring
        far_low, far_high = self.part(ring.far, 0), self.part(ring.far, 1)
        self.relay_r.wait_recv()
        self.pass_low = ring.send(far_low, far_low, ring.partner)
        self.relay_l.wait_recv()
        self.pass_high = ring.send(far_high, far_high, ring.partner)
        for copy in (self.own, self.pass_left, self.pass_right, self.pass_low, self.pass_high):
            copy.wait_recv()

    def sent(self):
        for copy in (self.r0, self.l1, self.r1, self.l0, self.own, self.relay_r, self.relay_l, self.pass_left,
                     self.pass_right, self.pass_low, self.pass_high):
            copy.wait_send()


class Reduce:
    def __init__(self, ring, part, bufs):
        self.ring, self.part = ring, part
        self.from_partner, self.sums, self.via_left, self.via_right, self.in_left, self.in_right = bufs
        self.half = ring.rows // 2
        self.chips = (ring.far_chip, ring.right_chip, ring.left_chip, ring.chip)

    def start(self):
        ring = self.ring
        self.swaps = []
        for slot, chip in enumerate(self.chips):
            rows = self.part.at[aligned(chip * 2 + 1 - ring.core, ring.rows)]
            self.swaps.append(ring.send(rows, self.from_partner.at[slot], ring.partner))

    def add(self, slot):
        self.swaps[slot].wait_recv()
        rows = aligned(self.chips[slot] * 2 + self.ring.core, self.ring.rows)
        self.sums[slot] = self.part[rows, :] + self.from_partner[slot]

    def far_out(self):
        ring, half = self.ring, self.half
        self.add(0)
        self.far_r = ring.send(self.sums.at[0, 0:half], self.via_left, ring.right)
        self.far_l = ring.send(self.sums.at[0, half:2 * half], self.via_right, ring.left)

    def near_out(self):
        ring, half = self.ring, self.half
        self.add(1)
        self.near_r = ring.send(self.sums.at[1, half:2 * half], self.in_left.at[half:2 * half], ring.right)
        self.add(2)
        self.near_l = ring.send(self.sums.at[2, 0:half], self.in_right.at[0:half], ring.left)
        self.add(3)

    def relay(self):
        ring, half = self.ring, self.half
        self.far_r.wait_recv()
        self.sums[1, 0:half] = self.sums[1, 0:half] + self.via_left[...]
        self.relay_r = ring.send(self.sums.at[1, 0:half], self.in_left.at[0:half], ring.right)
        self.far_l.wait_recv()
        self.sums[2, half:2 * half] = self.sums[2, half:2 * half] + self.via_right[...]
        self.relay_l = ring.send(self.sums.at[2, half:2 * half], self.in_right.at[half:2 * half], ring.left)

    def finish(self):
        for copy in (self.near_r, self.near_l, self.relay_r, self.relay_l):
            copy.wait_recv()
        return self.sums[3] + self.in_left[...] + self.in_right[...]

    def sent(self):
        for copy in (*self.swaps, self.far_r, self.far_l, self.near_r, self.near_l, self.relay_r, self.relay_l):
            copy.wait_send()


def reduce_scratch(rows, width):
    return [pltpu.VMEM((4, rows, width), F32), pltpu.VMEM((4, rows, width), F32),
            pltpu.VMEM((rows // 2, width), F32), pltpu.VMEM((rows // 2, width), F32),
            pltpu.VMEM((rows, width), F32), pltpu.VMEM((rows, width), F32)]


REDUCE_BUFS = 6


def norm_rows(row_vals, gain_vec):
    vals = row_vals.astype(F32)
    return (vals * lax.rsqrt(jnp.mean(vals * vals, axis=-1, keepdims=True) + NORM_EPS) * gain_vec).astype(BF16)


def norm_rows_backward(row_vals, gain_vec, cot_rows):
    vals = row_vals.astype(F32)
    scale = lax.rsqrt(jnp.mean(vals * vals, axis=-1, keepdims=True) + NORM_EPS)
    unit = vals * scale
    grad_gain = jnp.sum(cot_rows * unit, axis=0, keepdims=True)
    cot_unit = cot_rows * gain_vec
    grad_vals = scale * (cot_unit - unit * jnp.mean(cot_unit * unit, axis=-1, keepdims=True))
    return grad_vals, grad_gain


def head_probs(query, key, score_scale):
    seq_len = query.shape[0]
    scores = dot(query, key, NT) * score_scale
    row_pos = lax.broadcasted_iota(jnp.int32, (seq_len, seq_len), 0)
    col_pos = lax.broadcasted_iota(jnp.int32, (seq_len, seq_len), 1)
    scores = jnp.where(row_pos >= col_pos, scores, -1e30)
    exp_scores = jnp.exp(scores - jnp.max(scores, axis=-1, keepdims=True))
    return exp_scores / jnp.sum(exp_scores, axis=-1, keepdims=True)


def residual(row_vals, total):
    return (row_vals.astype(F32) + total.astype(BF16).astype(F32)).astype(BF16)


def loop(count, body):
    def step(index, carry):
        body(index)
        return carry
    lax.fori_loop(0, count, step, 0)


class AttentionBlock:
    def __init__(self, env, layer):
        self.env, self.layer = env, layer
        self.weights = ((env.w_qkv, env.qkv_w, env.grad_qkv_out), (env.w_out, env.out_w, env.grad_out_out))
        self.sems = (0, 1)
        self.rows_ref = env.layer_rows.at[layer]
        self.gain = env.gain_attn[layer:layer + 1, :]
        self.gain_row = layer
        self.scale = env.head_dim ** -0.5
        self.qkv = env.qkv.at[layer]
        self.mix = env.mix.at[layer]

    def cols(self, slot):
        return slice(slot * self.env.head_dim, (slot + 1) * self.env.head_dim)

    def gathered(self, micro):
        self.qkv[micro] = dot(self.env.full[...], self.env.qkv_w[...]).astype(BF16)

    def forward(self, micro):
        env = self.env
        key = self.qkv[micro, :, self.cols(env.groups)]
        value = self.qkv[micro, :, self.cols(env.groups + 1)]
        for head in range(env.groups):
            cols = self.cols(head)
            prob = head_probs(self.qkv[micro, :, cols], key, self.scale).astype(BF16)
            self.mix[micro, :, cols] = dot(prob, value).astype(BF16)

        def columns(index):
            cols = aligned(index, 512)
            env.part[micro, :, cols] = dot(self.mix[micro], env.out_w[:, cols])
        loop(env.out_w.shape[1] // 512, columns)

    def backward(self, micro, cot):
        env = self.env
        groups = env.groups
        env.grad_mix[...] = dot(cot[...], env.out_w[...], NT).astype(BF16)
        key = self.qkv[micro, :, self.cols(groups)]
        value = self.qkv[micro, :, self.cols(groups + 1)]
        grad_key = grad_value = None
        for head in range(groups):
            cols = self.cols(head)
            query = self.qkv[micro, :, cols]
            head_grad = env.grad_mix[:, cols]
            prob = head_probs(query, key, self.scale)
            grad_prob = dot(head_grad, value, NT).astype(BF16).astype(F32)
            row_dot = jnp.sum(grad_prob * prob, axis=-1, keepdims=True)
            grad_scores = (prob * (grad_prob - row_dot) * self.scale).astype(BF16)
            env.grad_qkv[:, cols] = dot(grad_scores, key).astype(BF16)
            key_term = dot(grad_scores, query, TN)
            value_term = dot(prob.astype(BF16), head_grad, TN)
            grad_key = key_term if grad_key is None else grad_key + key_term
            grad_value = value_term if grad_value is None else grad_value + value_term
        env.grad_qkv[:, self.cols(groups)] = grad_key.astype(BF16)
        env.grad_qkv[:, self.cols(groups + 1)] = grad_value.astype(BF16)

        def columns(index):
            cols = aligned(index, 256)
            env.part[micro, :, cols] = dot(env.grad_qkv[...], env.qkv_w[cols, :], NT)
        loop(env.qkv_w.shape[0] // 256, columns)

    def weights_near(self, micro):
        env = self.env

        def columns(index):
            cols = aligned(index, 256)
            env.put(micro, env.acc_qkv, env.qkv_w, cols, dot(env.full[:, cols], env.grad_qkv[...], TN))
        loop(env.full.shape[1] // 256, columns)
        return (0,) if micro else ()

    def weights_far(self, cots):
        env = self.env

        def columns(index):
            cols = aligned(index, 128)
            env.out_w[cols, :] = (dot(self.mix[0, :, cols], cots[0][...], TN)
                                  + dot(self.mix[1, :, cols], cots[1][...], TN)).astype(BF16)
        loop(env.out_w.shape[0] // 128, columns)
        return (1,)


class MlpBlock:
    def __init__(self, env, layer):
        self.env, self.layer = env, layer
        self.weights = ((env.w_gate, env.gate_w, env.grad_gate_out), (env.w_up, env.up_w, env.grad_up_out),
                        (env.w_down, env.down_w, env.grad_down_out))
        self.sems = (2, 3, 4)
        self.rows_ref = env.hidden_rows.at[layer]
        self.gain = env.gain_mlp[layer:layer + 1, :]
        self.gain_row = env.layers + layer

    def gathered(self, micro):
        env = self.env

        def columns(index):
            cols = aligned(index, 256)
            gate_pre = dot(env.full[...], env.gate_w[:, cols])
            up_proj = dot(env.full[...], env.up_w[:, cols])
            env.inner[micro, :, cols] = (gate_pre * jax.nn.sigmoid(gate_pre) * up_proj).astype(BF16)
        loop(env.gate_w.shape[1] // 256, columns)

    def forward(self, micro):
        env = self.env

        def columns(index):
            cols = aligned(index, 512)
            env.part[micro, :, cols] = dot(env.inner[micro], env.down_w[:, cols])
        loop(env.down_w.shape[1] // 512, columns)

    def backward(self, micro, cot):
        env = self.env

        def columns(index):
            cols = aligned(index, 256)
            gate_pre = dot(env.full[...], env.gate_w[:, cols])
            up_proj = dot(env.full[...], env.up_w[:, cols])
            grad_inner = dot(cot[...], env.down_w[cols, :], NT).astype(BF16).astype(F32)
            gate_sig = jax.nn.sigmoid(gate_pre)
            gate_act = gate_pre * gate_sig
            env.inner[micro, :, cols] = (gate_act * up_proj).astype(BF16)
            env.grad_up[:, cols] = (grad_inner * gate_act).astype(BF16)
            env.grad_gate[:, cols] = (grad_inner * up_proj * gate_sig * (1.0 + gate_pre * (1.0 - gate_sig))).astype(BF16)
        loop(env.gate_w.shape[1] // 256, columns)

        def out_columns(index):
            cols = aligned(index, 256)
            env.part[micro, :, cols] = (dot(env.grad_gate[...], env.gate_w[cols, :], NT)
                                        + dot(env.grad_up[...], env.up_w[cols, :], NT))
        loop(env.gate_w.shape[0] // 256, out_columns)

    def weights_near(self, micro):
        env = self.env

        def columns(index):
            cols = aligned(index, 256)
            env.put(micro, env.acc_gate, env.gate_w, cols, dot(env.full[:, cols], env.grad_gate[...], TN))
            env.put(micro, env.acc_up, env.up_w, cols, dot(env.full[:, cols], env.grad_up[...], TN))
        loop(env.full.shape[1] // 256, columns)
        return (0, 1) if micro else ()

    def weights_far(self, cots):
        env = self.env

        def columns(index):
            cols = aligned(index, 128)
            env.down_w[cols, :] = (dot(env.inner[0, :, cols], cots[0][...], TN)
                                   + dot(env.inner[1, :, cols], cots[1][...], TN)).astype(BF16)
        loop(env.down_w.shape[0] // 128, columns)
        return (2,)


FORWARD_ORDER = 'XEfrnR'
BACKWARD_ORDER = 'EXrfwVnRvW'


class Env:
    def __init__(self, names, refs, **sizes):
        self.__dict__.update(zip(names, refs))
        self.__dict__.update(sizes)

    def put(self, micro, acc, stage, rows, term):
        if micro == 0:
            acc[rows, :] = term
        else:
            stage[rows, :] = (acc[rows, :] + term).astype(BF16)


def stack_kernel(names, sizes, *refs):
    env = Env(names, refs, **sizes)
    layers, devices = env.layers, env.devices
    ring = Ring(devices, env.x_in.shape[1], env.send_sems, env.recv_sems)
    own = aligned(ring.me, ring.rows)
    blocks = []
    for layer in range(layers):
        blocks += [AttentionBlock(env, layer), MlpBlock(env, layer)]

    def load(block):
        copies = [pltpu.make_async_copy(src.at[block.layer], dst, env.load_sems.at[sem])
                  for (src, dst, unused), sem in zip(block.weights, block.sems)]
        for copy in copies:
            copy.start()
        return copies

    stores = {}
    loads = {block: load(block) for block in blocks[:2]}

    def need(block):
        for copy in loads.pop(block, ()):
            copy.wait()

    def store(block, indices):
        for index in indices:
            unused, src, dst = block.weights[index]
            copy = pltpu.make_async_copy(src, dst.at[block.layer], env.store_sems.at[block.sems[index]])
            copy.start()
            stores.setdefault(block, []).append(copy)

    barrier = pltpu.get_barrier_semaphore()
    others = [lax.rem(ring.me + step, devices) for step in range(1, devices)]
    for peer in others:
        pl.semaphore_signal(barrier, inc=1, device_id={'tp': peer}, device_id_type=MESH)
    pl.semaphore_wait(barrier, len(others))

    uses = []

    def full_start(block, micro):
        if uses:
            pl.semaphore_wait(env.credit, len(ring.peers))
        uses.append(block)
        env.full[own, :] = norm_rows(block.rows_ref[micro], block.gain)
        ring.used = 0
        gather = Gather(ring, env.full)
        gather.start()
        ring.used = AG_COPIES
        return gather

    def resume(index):
        ring.used = index

    total_uses = 2 * len(blocks) * 2

    def full_done(gather):
        gather.sent()
        if len(uses) < total_uses:
            for peer in ring.peers:
                pl.semaphore_signal(env.credit, inc=1, device_id={'tp': peer}, device_id_type=MESH)

    def gather_base(micro):
        return AG_COPIES * (1 + micro)

    def reduce_base(micro):
        return AG_COPIES * 3 + RS_COPIES * micro

    def staged(base, start, step):
        resume(base + start)
        return step()

    def relay(gather, base):
        staged(base, 5, gather.relay)

    def finish(gather, base):
        staged(base, 9, gather.finish)

    reducers = [None, None]

    def reduce_start(micro):
        reducer = Reduce(ring, env.part.at[micro], tuple(buf.at[micro] for buf in (
            env.from_partner, env.sums, env.via_left, env.via_right, env.in_left, env.in_right)))
        reducers[micro] = reducer
        staged(reduce_base(micro), 0, reducer.start)

    def reduce_far(micro):
        staged(reduce_base(micro), 4, reducers[micro].far_out)

    def reduce_near(micro):
        staged(reduce_base(micro), 6, reducers[micro].near_out)

    def reduce_relay(micro):
        staged(reduce_base(micro), 8, reducers[micro].relay)

    def reduce_finish(micro):
        total = reducers[micro].finish()
        reducers[micro].sent()
        reducers[micro] = None
        return total

    def after_forward(index, micro):
        total = reduce_finish(micro)
        block = blocks[index]
        rows = residual(block.rows_ref[micro], total)
        if index + 1 < len(blocks):
            blocks[index + 1].rows_ref[micro] = rows
        else:
            env.y_out[micro] = rows

    for micro in range(2):
        blocks[0].rows_ref[micro] = env.x_in[micro]
    back = blocks[::-1]
    cot_rows = env.cot_rows
    for micro in range(2):
        cot_rows[0, micro] = env.y_cot[micro]
    cot_gathers = [None, None]

    def cot_start(index, micro):
        cots = env.cots.at[index % 2, micro]
        cots[own, :] = cot_rows[index % 2, micro]
        resume(gather_base(micro))
        cot_gathers[micro] = Gather(ring, cots)
        cot_gathers[micro].start()

    gather = full_start(blocks[0], 0)
    relay(gather, 0)
    for index, block in enumerate(blocks):
        last = index + 1 == len(blocks)
        for micro in range(2):
            finish(gather, 0)
            need(block)
            block.gathered(micro)
            full_done(gather)
            for step in FORWARD_ORDER:
                if step == 'X':
                    block.forward(micro)
                    reduce_start(micro)
                elif step == 'E':
                    if micro == 0:
                        if index > 0:
                            after_forward(index - 1, 1)
                        gather = full_start(block, 1)
                    else:
                        after_forward(index, 0)
                        if last:
                            cot_start(0, 0)
                        gather = full_start(back[0] if last else blocks[index + 1], 0)
                elif step == 'f':
                    reduce_far(micro)
                elif step == 'r':
                    if last and micro == 1:
                        relay(cot_gathers[0], gather_base(0))
                    relay(gather, 0)
                elif step == 'n':
                    reduce_near(micro)
                else:
                    reduce_relay(micro)
        if index + 2 < len(blocks):
            loads[blocks[index + 2]] = load(blocks[index + 2])

    def after_backward(index, micro):
        total = reduce_finish(micro).astype(BF16).astype(F32)
        block = back[index]
        grad_rows, grad_gain = norm_rows_backward(block.rows_ref[micro], block.gain, total)
        rows = (cot_rows[index % 2, micro].astype(F32) + grad_rows).astype(BF16)
        gain_row = slice(block.gain_row, block.gain_row + 1)
        env.gains[gain_row, :] = grad_gain if micro == 0 else env.gains[gain_row, :] + grad_gain
        if index + 1 < len(back):
            cot_rows[(index + 1) % 2, micro] = rows
        else:
            env.grad_x[micro] = rows

    for index, block in enumerate(back):
        last = index + 1 == len(back)
        for micro in range(2):
            other = 1 - micro
            finish(cot_gathers[micro], gather_base(micro))
            finish(gather, 0)
            need(block)
            going = micro == 0 or not last
            for step in BACKWARD_ORDER:
                if step == 'X':
                    block.backward(micro, env.cots.at[index % 2, micro])
                    reduce_start(micro)
                elif step == 'E':
                    if micro == 1:
                        after_backward(index, 0)
                    elif index == 0:
                        after_forward(len(blocks) - 1, 1)
                    else:
                        after_backward(index - 1, 1)
                    if going:
                        cot_start(index + micro, other)
                elif step == 'f':
                    reduce_far(micro)
                elif step == 'w':
                    store(block, block.weights_near(micro))
                    full_done(gather)
                    cot_gathers[micro].sent()
                elif step == 'r':
                    if going:
                        relay(cot_gathers[other], gather_base(other))
                elif step == 'V':
                    if going:
                        gather = full_start(block if micro == 0 else back[index + 1], other)
                elif step == 'n':
                    reduce_near(micro)
                elif step == 'R':
                    reduce_relay(micro)
                elif step == 'v':
                    if going:
                        relay(gather, 0)
                elif micro == 1:
                    store(block, block.weights_far([env.cots.at[index % 2, 0], env.cots.at[index % 2, 1]]))
                elif index > 0 and not last:
                    for copy in stores.pop(back[index - 1], ()):
                        copy.wait()
                    loads[back[index + 1]] = load(back[index + 1])
    after_backward(len(back) - 1, 1)

    copies = []
    for index, peer in enumerate(others):
        copy = pltpu.make_async_remote_copy(env.gains, env.gain_parts.at[ring.me], env.gain_send.at[index],
                                            env.gain_recv.at[index], device_id={'tp': peer}, device_id_type=MESH)
        copy.start()
        copies.append(copy)
    env.gain_parts[ring.me] = env.gains[...]
    for copy in copies:
        copy.wait()
    total = env.gain_parts[0]
    for index in range(1, devices):
        total = total + env.gain_parts[index]
    env.gain_out[...] = total
    for copies in stores.values():
        for copy in copies:
            copy.wait()


def comm_params(collective_id):
    return pltpu.CompilerParams(collective_id=collective_id, has_side_effects=True, vmem_limit_bytes=66_000_000)


def solution(mesh):
    devices = mesh.shape['tp']
    row_spec = P(None, ('dp', 'tp'), None)
    gain_spec = P(None, None)
    qkv_spec = P(None, None, 'tp', None, None)
    head_spec = P(None, 'tp', None, None)
    col_spec = P(None, None, 'tp')
    row_shard_spec = P(None, 'tp', None)

    def device_program(x_in, y_cot, gain_attn, gain_mlp, w_qkv, w_out, w_gate, w_up, w_down):
        micros, rows, width = x_in.shape
        layers = w_qkv.shape[0]
        groups = w_qkv.shape[3] - 2
        head_dim = w_qkv.shape[4]
        seq_len = rows * devices
        qkv_width = (groups + 2) * head_dim
        mix_width = groups * head_dim
        inner_width = w_gate.shape[2]
        inputs = {
            'x_in': (x_in, VMEM), 'y_cot': (y_cot, VMEM), 'gain_attn': (gain_attn, VMEM), 'gain_mlp': (gain_mlp, VMEM),
            'w_qkv': (w_qkv.reshape(layers, width, qkv_width), ANY), 'w_out': (w_out.reshape(layers, mix_width, width), ANY),
            'w_gate': (w_gate, ANY), 'w_up': (w_up, ANY), 'w_down': (w_down, ANY)}

        def out(shape, dtype, spec):
            return jax.ShapeDtypeStruct(shape, dtype), spec

        outputs = {
            'y_out': out(x_in.shape, BF16, VMEM), 'grad_x': out(x_in.shape, BF16, VMEM),
            'grad_qkv_out': out((layers, width, qkv_width), BF16, ANY), 'grad_out_out': out((layers, mix_width, width), BF16, ANY),
            'grad_gate_out': out(w_gate.shape, BF16, ANY), 'grad_up_out': out(w_up.shape, BF16, ANY),
            'grad_down_out': out(w_down.shape, BF16, ANY), 'gain_out': out((2 * layers, width), F32, VMEM)}

        def bf16(*shape):
            return pltpu.VMEM(shape, BF16)

        def f32(*shape):
            return pltpu.VMEM(shape, F32)

        def dma(count):
            return pltpu.SemaphoreType.DMA((count,))

        copies = 3 * AG_COPIES + 2 * RS_COPIES
        scratch = {
            'layer_rows': bf16(layers, micros, rows, width), 'hidden_rows': bf16(layers, micros, rows, width),
            'cot_rows': bf16(2, micros, rows, width), 'qkv': bf16(layers, micros, seq_len, qkv_width),
            'mix': bf16(layers, micros, seq_len, mix_width), 'inner': bf16(micros, seq_len, inner_width),
            'grad_gate': bf16(seq_len, inner_width), 'grad_up': bf16(seq_len, inner_width),
            'grad_mix': bf16(seq_len, mix_width), 'grad_qkv': bf16(seq_len, qkv_width),
            'qkv_w': bf16(width, qkv_width), 'out_w': bf16(mix_width, width), 'gate_w': bf16(width, inner_width),
            'up_w': bf16(width, inner_width), 'down_w': bf16(inner_width, width),
            'acc_qkv': f32(width, qkv_width), 'acc_gate': f32(width, inner_width), 'acc_up': f32(width, inner_width),
            'full': bf16(seq_len, width), 'cots': bf16(2, micros, seq_len, width), 'part': f32(micros, seq_len, width),
            'from_partner': f32(micros, 4, rows, width), 'sums': f32(micros, 4, rows, width),
            'via_left': f32(micros, rows // 2, width), 'via_right': f32(micros, rows // 2, width),
            'in_left': f32(micros, rows, width), 'in_right': f32(micros, rows, width),
            'gains': f32(2 * layers, width), 'gain_parts': f32(devices, 2 * layers, width),
            'load_sems': dma(5), 'store_sems': dma(5), 'send_sems': dma(copies), 'recv_sems': dma(copies),
            'gain_send': dma(devices - 1), 'gain_recv': dma(devices - 1), 'credit': pltpu.SemaphoreType.REGULAR}
        names = (*inputs, *outputs, *scratch)
        sizes = dict(layers=layers, devices=devices, groups=groups, head_dim=head_dim)
        results = pl.pallas_call(
            functools.partial(stack_kernel, names, sizes),
            out_shape=tuple(shape for shape, spec in outputs.values()),
            in_specs=[spec for array, spec in inputs.values()], out_specs=tuple(spec for shape, spec in outputs.values()),
            scratch_shapes=list(scratch.values()), compiler_params=comm_params(0), name='stack',
        )(*(array for array, spec in inputs.values()))
        y_rows, grad_rows, grad_qkv, grad_out, grad_gate, grad_up, grad_down, gain_sum = results
        return (y_rows, grad_rows, grad_qkv.reshape(w_qkv.shape), grad_out.reshape(w_out.shape), grad_gate, grad_up, grad_down,
                gain_sum[:layers], gain_sum[layers:])

    return jax.shard_map(device_program, mesh=mesh,
                         in_specs=(row_spec, row_spec, gain_spec, gain_spec, qkv_spec, head_spec, col_spec, col_spec, row_shard_spec),
                         out_specs=(row_spec, row_spec, P('dp', None, 'tp', None, None), P('dp', 'tp', None, None), P('dp', None, 'tp'), P('dp', None, 'tp'), P('dp', 'tp', None), P('dp', None), P('dp', None)),
                         check_vma=False)
```

time: 958 us -> 367 us (0.38); the launches traced: 947 us -> 366 us
  waiting for transfers between devices: 607 us -> 0 us
  Pallas kernels: 0 us -> 335 us
  matrix products: 196 us -> 0 us
  other arithmetic: 52.4 us -> 0.01 us
  blocking collectives: 21.2 us -> 0 us
  local copies, waits for them, and re-layouts: 50.4 us -> 30.7 us
  between operations: 16.4 us -> 0.69 us
    reduce_scatter x16 -> x0, waiting for transfers between devices: 352 us -> none  [the longest x4 111 us: device_program(): lax.psum_scatter(down_part, 'tp', scatter_dimension=0, tiled=True)]
    pallas_call x0 -> x1, Pallas kernels: none -> 335 us  [device_program(): pl.pallas_call(functools.partial(stack_kernel, names, sizes), out_shape=t...]
    all_gather x16 -> x0, waiting for transfers between devices: 249 us -> none  [the longest x4 78.7 us: device_program(): normed_full = lax.all_gather(normed, 'tp', axis=0, tiled=True)]
    dot_general x84 -> x0, matrix products: 196 us -> none  [the longest x4 16 us: device_program(): jnp.einsum('sd,fd->sf', grad_full, w_down[layer_idx], preferred_element_t...]
    unnamed x317 -> x20, local copies, waits for them, and re-layouts: 42.7 us -> 15.1 us
    psum x1 -> x0, blocking collectives: 21.2 us -> none  [device_program(): lax.psum(jnp.stack([jnp.stack(gain_a_acc), jnp.stack(gain_b_acc)]), 'tp')]
    reduce_sum x15 -> x0, other arithmetic: 17.8 us -> none  [the longest x5 9.3 us: rms_scale(): row_vals * lax.rsqrt(jnp.mean(row_vals * row_vals, axis=-1, keepdims=True...]
    another operation x9 -> x0, other arithmetic: 15.8 us -> none  [the longest x1 6.16 us: device_program(): jnp.stack([item.astype(jnp.bfloat16) for item in grad_down_acc])]
  transfers between devices with their start and end apart: 32 -> 0, of which waited for: 29 -> 0; matrix products, arithmetic and copies ran while one was open for 25% -> 0% of each run, Pallas kernels for 0% -> 0%
where the time goes in v2:
time: 367 us; the launch traced here: 366 us
  Pallas kernels  335 us (91%)
  local copies, waits for them, and re-layouts  30.7 us (8%)
    pallas_call x1, Pallas kernels, device_program(): pl.pallas_call(functools.partial(stack_kernel, names, sizes), out_shape=t...  335 us
    unnamed x20, local copies, waits for them, and re-layouts  15.1 us

profile of v2, /device:TPU:81, one launch (start us, length us, event | category | flops | bytes accessed | tf_op | source)
XLA Modules:
  0.0 366.3 jit_solution(11641825216535338457)
XLA Ops:
  0.6 7.2 %reshape.30.refs_4_ = bf16[2,2048,512]{2,1,0:T(8,128)(2,1)} reshape(bf16[2,2048,1,4,128]{4,3,2,1,0:T(4,128)(2,1)} %param.13) | data formatting | bytes 8388608 | tf_op jit(solution)/shard_map/reshape | solution.py:637
  7.8 334.8 %stack.1 = (bf16[2,32,2048]{2,1,0:T(8,128)(2,1)}, bf16[2,32,2048]{2,1,0:T(8,128)(2,1)}, bf16[2,2048,512]{2,1,0:T(8,128)(2,1)}, bf16[2,256,2048]{2,1,0:T(8,128)(2...) custom-call(bf16[2,32,2048]{2,1,0:T(8,128)(2,1)} %refs_0_.1, ...), custom_call_target="tpu_custom_call" | custom-call | tf_op jit(solution)/shard_map/stack/pallas_call | solution.py:677
  342.6 0.0 copy-start.2
  342.6 0.0 copy-start.1
  342.7 0.0 copy-start
  342.7 1.5 fusion
  344.2 6.9 %reshape.32 = bf16[2,2048,1,4,128]{4,3,1,0,2:T(4,128)(2,1)} reshape(bf16[2,2048,512]{2,1,0:T(8,128)(2,1)} %get-tuple-element.19) | data formatting | bytes 8388608 | tf_op jit(solution)/shard_map/reshape | solution.py:684
  351.1 0.0 copy-done.2
  351.1 0.7 copy.25
  351.8 0.0 copy-done.1
  351.8 0.7 copy.26
  352.5 0.0 copy-done
  352.5 0.0 slice-start.2
  352.5 1.3 copy.27
  353.8 0.0 slice-start.3
  353.8 0.0 slice-start
  353.8 6.6 %copy.28 = bf16[2,2048,768]{2,1,0:T(8,128)(2,1)} copy(bf16[2,2048,768]{2,1,0:T(8,128)(2,1)} %get-tuple-element.49) | data formatting | bytes 12582912
  360.4 0.0 slice-done.2
  360.4 0.0 slice-done.3
  360.4 0.0 slice-start.1
  360.4 2.8 copy.29
  363.3 0.0 slice-done
  363.3 0.3 slice-done.1
  363.5 2.7 copy.30
  (2 shorter events, 0.0 us)
Async XLA Ops:
  342.6 8.5 %copy-start.2 = (bf16[2,32,2048]{2,1,0:T(8,128)(2,1)S(1)}, bf16[2,32,2048]{2,1,0:T(8,128)(2,1)}, u32[]{:S(2)}) copy-start(bf16[2,32,2048]{2,1,0:T(8,128)(2,1)} %get-tuple-element.45) | copy-start | bytes 786436
  342.6 9.2 %copy-start.1 = (bf16[2,32,2048]{2,1,0:T(8,128)(2,1)S(1)}, bf16[2,32,2048]{2,1,0:T(8,128)(2,1)}, u32[]{:S(2)}) copy-start(bf16[2,32,2048]{2,1,0:T(8,128)(2,1)} %get-tuple-element.46) | copy-start | bytes 786436
  342.7 9.9 %copy-start = (bf16[2,256,2048]{2,1,0:T(8,128)(2,1)S(1)}, bf16[2,256,2048]{2,1,0:T(8,128)(2,1)}, u32[]{:S(2)}) copy-start(bf16[2,256,2048]{2,1,0:T(8,128)(2,1)} %get-tuple-element.20) | copy-start | bytes 6291460
  352.5 7.9 %slice-start.2 = ((s8[6291456]{0:T(1024)(128)(4,1)}), s8[4194304]{0:T(1024)(128)(4,1)S(1)}, s32[]{:S(2)}) async-start(s8[6291456]{0:T(1024)(128)(4,1)} %bitcast.5), calls=%async_computation.2 | async-start | bytes 8388608
  353.8 6.6 %slice-start.3 = ((s8[6291456]{0:T(1024)(128)(4,1)}), s8[2097152]{0:T(1024)(128)(4,1)S(1)}, s32[]{:S(2)}) async-start(s8[6291456]{0:T(1024)(128)(4,1)} %bitcast.5), calls=%async_computation.3 | async-start | bytes 4194304
  353.8 9.4 %slice-start = ((s8[6291456]{0:T(1024)(128)(4,1)}), s8[4194304]{0:T(1024)(128)(4,1)S(1)}, s32[]{:S(2)}) async-start(s8[6291456]{0:T(1024)(128)(4,1)} %bitcast.3), calls=%async_computation | async-start | bytes 8388608
  360.4 3.1 slice-start.1

commit v3 on v2

--- a/solution.py
+++ b/solution.py
@@ -15,6 +15,7 @@
 VMEM = pl.BlockSpec(memory_space=pltpu.VMEM)
 AG_COPIES = 11
 RS_COPIES = 10
+HALVES = 1
 NN = (((1,), (0,)), ((), ()))
 NT = (((1,), (1,)), ((), ()))
 TN = (((0,), (0,)), ((), ()))
@@ -176,14 +177,15 @@
     return (vals * lax.rsqrt(jnp.mean(vals * vals, axis=-1, keepdims=True) + NORM_EPS) * gain_vec).astype(BF16)
 
 
-def norm_rows_backward(row_vals, gain_vec, cot_rows):
+def norm_unit(row_vals):
     vals = row_vals.astype(F32)
     scale = lax.rsqrt(jnp.mean(vals * vals, axis=-1, keepdims=True) + NORM_EPS)
-    unit = vals * scale
-    grad_gain = jnp.sum(cot_rows * unit, axis=0, keepdims=True)
+    return vals * scale, scale
+
+
+def norm_rows_backward(unit, scale, gain_vec, cot_rows):
     cot_unit = cot_rows * gain_vec
-    grad_vals = scale * (cot_unit - unit * jnp.mean(cot_unit * unit, axis=-1, keepdims=True))
-    return grad_vals, grad_gain
+    return scale * (cot_unit - unit * jnp.mean(cot_unit * unit, axis=-1, keepdims=True))
 
 
 def head_probs(query, key, score_scale):
@@ -210,7 +212,9 @@
 class AttentionBlock:
     def __init__(self, env, layer):
         self.env, self.layer = env, layer
-        self.weights = ((env.w_qkv, env.qkv_w, env.grad_qkv_out), (env.w_out, env.out_w, env.grad_out_out))
+        self.weights = ((env.stage_qkv, env.grad_qkv_out), (env.out_w, env.grad_out_out))
+        self.loads = [(env.w_qkv.at[layer], env.qkv_w), (env.w_out.at[layer], env.out_w)]
+        self.load_base = 3
         self.sems = (0, 1)
         self.rows_ref = env.layer_rows.at[layer]
         self.gain = env.gain_attn[layer:layer + 1, :]
@@ -234,9 +238,12 @@
             prob = head_probs(self.qkv[micro, :, cols], key, self.scale).astype(BF16)
             self.mix[micro, :, cols] = dot(prob, value).astype(BF16)
 
+    def forward_partial(self, micro, half):
+        env = self.env
+
         def columns(index):
             cols = aligned(index, 512)
-            env.part[micro, :, cols] = dot(self.mix[micro], env.out_w[:, cols])
+            env.part[micro, half, :, cols] = dot(self.mix[micro], env.out_w[:, cols])
         loop(env.out_w.shape[1] // 512, columns)
 
     def backward(self, micro, cot):
@@ -262,19 +269,22 @@
         env.grad_qkv[:, self.cols(groups)] = grad_key.astype(BF16)
         env.grad_qkv[:, self.cols(groups + 1)] = grad_value.astype(BF16)
 
+    def backward_partial(self, micro, half):
+        env = self.env
+
         def columns(index):
             cols = aligned(index, 256)
-            env.part[micro, :, cols] = dot(env.grad_qkv[...], env.qkv_w[cols, :], NT)
+            env.part[micro, half, :, cols] = dot(env.grad_qkv[...], env.qkv_w[cols, :], NT)
         loop(env.qkv_w.shape[0] // 256, columns)
 
-    def weights_near(self, micro):
+    def weights_near(self, second):
         env = self.env
 
         def columns(index):
             cols = aligned(index, 256)
-            env.put(micro, env.acc_qkv, env.qkv_w, cols, dot(env.full[:, cols], env.grad_qkv[...], TN))
+            env.put(second, env.acc_qkv, env.stage_qkv, cols, dot(env.full[:, cols], env.grad_qkv[...], TN))
         loop(env.full.shape[1] // 256, columns)
-        return (0,) if micro else ()
+        return (0,) if second else ()
 
     def weights_far(self, cots):
         env = self.env
@@ -290,8 +300,9 @@
 class MlpBlock:
     def __init__(self, env, layer):
         self.env, self.layer = env, layer
-        self.weights = ((env.w_gate, env.gate_w, env.grad_gate_out), (env.w_up, env.up_w, env.grad_up_out),
-                        (env.w_down, env.down_w, env.grad_down_out))
+        self.weights = ((env.stage_gate, env.grad_gate_out), (env.stage_up, env.grad_up_out), (env.down_w, env.grad_down_out))
+        self.loads = [(env.w_gate.at[layer], env.gate_w), (env.w_up.at[layer], env.up_w), (env.w_down.at[layer], env.down_w)]
+        self.load_base = 0
         self.sems = (2, 3, 4)
         self.rows_ref = env.hidden_rows.at[layer]
         self.gain = env.gain_mlp[layer:layer + 1, :]
@@ -308,11 +319,14 @@
         loop(env.gate_w.shape[1] // 256, columns)
 
     def forward(self, micro):
+        pass
+
+    def forward_partial(self, micro, half):
         env = self.env
 
         def columns(index):
             cols = aligned(index, 512)
-            env.part[micro, :, cols] = dot(env.inner[micro], env.down_w[:, cols])
+            env.part[micro, half, :, cols] = dot(env.inner[micro], env.down_w[:, cols])
         loop(env.down_w.shape[1] // 512, columns)
 
     def backward(self, micro, cot):
@@ -330,21 +344,24 @@
             env.grad_gate[:, cols] = (grad_inner * up_proj * gate_sig * (1.0 + gate_pre * (1.0 - gate_sig))).astype(BF16)
         loop(env.gate_w.shape[1] // 256, columns)
 
-        def out_columns(index):
+    def backward_partial(self, micro, half):
+        env = self.env
+
+        def columns(index):
             cols = aligned(index, 256)
-            env.part[micro, :, cols] = (dot(env.grad_gate[...], env.gate_w[cols, :], NT)
-                                        + dot(env.grad_up[...], env.up_w[cols, :], NT))
-        loop(env.gate_w.shape[0] // 256, out_columns)
-
-    def weights_near(self, micro):
+            env.part[micro, half, :, cols] = (dot(env.grad_gate[...], env.gate_w[cols, :], NT)
+                                              + dot(env.grad_up[...], env.up_w[cols, :], NT))
+        loop(env.gate_w.shape[0] // 256, columns)
+
+    def weights_near(self, second):
         env = self.env
 
         def columns(index):
             cols = aligned(index, 256)
-            env.put(micro, env.acc_gate, env.gate_w, cols, dot(env.full[:, cols], env.grad_gate[...], TN))
-            env.put(micro, env.acc_up, env.up_w, cols, dot(env.full[:, cols], env.grad_up[...], TN))
+            env.put(second, env.acc_gate, env.stage_gate, cols, dot(env.full[:, cols], env.grad_gate[...], TN))
+            env.put(second, env.acc_up, env.stage_up, cols, dot(env.full[:, cols], env.grad_up[...], TN))
         loop(env.full.shape[1] // 256, columns)
-        return (0, 1) if micro else ()
+        return (0, 1) if second else ()
 
     def weights_far(self, cots):
         env = self.env
@@ -358,7 +375,7 @@
 
 
 FORWARD_ORDER = 'XEfrnR'
-BACKWARD_ORDER = 'EXrfwVnRvW'
+BACKWARD_ORDER = 'XwEVPfrvnRW'
 
 
 class Env:
@@ -366,11 +383,11 @@
         self.__dict__.update(zip(names, refs))
         self.__dict__.update(sizes)
 
-    def put(self, micro, acc, stage, rows, term):
-        if micro == 0:
+    def put(self, second, acc, stage, rows, term):
+        if second:
+            stage[rows, :] = (acc[rows, :] + term).astype(BF16)
+        else:
             acc[rows, :] = term
-        else:
-            stage[rows, :] = (acc[rows, :] + term).astype(BF16)
 
 
 def stack_kernel(names, sizes, *refs):
@@ -383,8 +400,8 @@
         blocks += [AttentionBlock(env, layer), MlpBlock(env, layer)]
 
     def load(block):
-        copies = [pltpu.make_async_copy(src.at[block.layer], dst, env.load_sems.at[sem])
-                  for (src, dst, unused), sem in zip(block.weights, block.sems)]
+        copies = [pltpu.make_async_copy(src, dst, env.load_sems.at[block.load_base + index])
+                  for index, (src, dst) in enumerate(block.loads)]
         for copy in copies:
             copy.start()
         return copies
@@ -398,7 +415,7 @@
 
     def store(block, indices):
         for index in indices:
-            unused, src, dst = block.weights[index]
+            src, dst = block.weights[index]
             copy = pltpu.make_async_copy(src, dst.at[block.layer], env.store_sems.at[block.sems[index]])
             copy.start()
             stores.setdefault(block, []).append(copy)
@@ -425,7 +442,7 @@
     def resume(index):
         ring.used = index
 
-    total_uses = 2 * len(blocks) * 2
+    total_uses = 4 * len(blocks) - 1
 
     def full_done(gather):
         gather.sent()
@@ -437,7 +454,7 @@
         return AG_COPIES * (1 + micro)
 
     def reduce_base(micro):
-        return AG_COPIES * 3 + RS_COPIES * micro
+        return AG_COPIES * 3 + RS_COPIES * HALVES * micro
 
     def staged(base, start, step):
         resume(base + start)
@@ -451,24 +468,31 @@
 
     reducers = [None, None]
 
-    def reduce_start(micro):
-        reducer = Reduce(ring, env.part.at[micro], tuple(buf.at[micro] for buf in (
-            env.from_partner, env.sums, env.via_left, env.via_right, env.in_left, env.in_right)))
-        reducers[micro] = reducer
-        staged(reduce_base(micro), 0, reducer.start)
+    def reduce_start(micro, partial):
+        reducers[micro] = []
+        for half in range(HALVES):
+            partial(micro, half)
+            reducer = Reduce(ring, env.part.at[micro, half], tuple(buf.at[micro, half] for buf in (
+                env.from_partner, env.sums, env.via_left, env.via_right, env.in_left, env.in_right)))
+            reducers[micro].append(reducer)
+            staged(reduce_base(micro) + RS_COPIES * half, 0, reducer.start)
 
     def reduce_far(micro):
-        staged(reduce_base(micro), 4, reducers[micro].far_out)
+        for half, reducer in enumerate(reducers[micro]):
+            staged(reduce_base(micro) + RS_COPIES * half, 4, reducer.far_out)
 
     def reduce_near(micro):
-        staged(reduce_base(micro), 6, reducers[micro].near_out)
+        for half, reducer in enumerate(reducers[micro]):
+            staged(reduce_base(micro) + RS_COPIES * half, 6, reducer.near_out)
 
     def reduce_relay(micro):
-        staged(reduce_base(micro), 8, reducers[micro].relay)
+        for half, reducer in enumerate(reducers[micro]):
+            staged(reduce_base(micro) + RS_COPIES * half, 8, reducer.relay)
 
     def reduce_finish(micro):
-        total = reducers[micro].finish()
-        reducers[micro].sent()
+        reducer, = reducers[micro]
+        total = reducer.finish()
+        reducer.sent()
         reducers[micro] = None
         return total
 
@@ -504,27 +528,32 @@
             finish(gather, 0)
             need(block)
             block.gathered(micro)
-            full_done(gather)
+            if not last or micro == 0:
+                full_done(gather)
             for step in FORWARD_ORDER:
                 if step == 'X':
                     block.forward(micro)
-                    reduce_start(micro)
+                    reduce_start(micro, block.forward_partial)
                 elif step == 'E':
                     if micro == 0:
                         if index > 0:
                             after_forward(index - 1, 1)
                         gather = full_start(block, 1)
                     else:
+                        if last:
+                            cot_start(0, 1)
                         after_forward(index, 0)
                         if last:
                             cot_start(0, 0)
-                        gather = full_start(back[0] if last else blocks[index + 1], 0)
+                        else:
+                            gather = full_start(blocks[index + 1], 0)
                 elif step == 'f':
                     reduce_far(micro)
                 elif step == 'r':
                     if last and micro == 1:
-                        relay(cot_gathers[0], gather_base(0))
-                    relay(gather, 0)
+                        relay(cot_gathers[1], gather_base(1))
+                    else:
+                        relay(gather, 0)
                 elif step == 'n':
                     reduce_near(micro)
                 else:
@@ -533,42 +562,47 @@
             loads[blocks[index + 2]] = load(blocks[index + 2])
 
     def after_backward(index, micro):
+        block = back[index]
+        unit, scale = norm_unit(block.rows_ref[micro])
         total = reduce_finish(micro).astype(BF16).astype(F32)
-        block = back[index]
-        grad_rows, grad_gain = norm_rows_backward(block.rows_ref[micro], block.gain, total)
-        rows = (cot_rows[index % 2, micro].astype(F32) + grad_rows).astype(BF16)
-        gain_row = slice(block.gain_row, block.gain_row + 1)
-        env.gains[gain_row, :] = grad_gain if micro == 0 else env.gains[gain_row, :] + grad_gain
+        rows = (cot_rows[index % 2, micro].astype(F32) + norm_rows_backward(unit, scale, block.gain, total)).astype(BF16)
         if index + 1 < len(back):
             cot_rows[(index + 1) % 2, micro] = rows
+            cot_start(index + 1, micro)
         else:
             env.grad_x[micro] = rows
+        gain_row = slice(block.gain_row, block.gain_row + 1)
+        grad_gain = jnp.sum(total * unit, axis=0, keepdims=True)
+        env.gains[gain_row, :] = grad_gain if micro == 1 else env.gains[gain_row, :] + grad_gain
 
     for index, block in enumerate(back):
         last = index + 1 == len(back)
-        for micro in range(2):
-            other = 1 - micro
+        for second in (False, True):
+            micro, other = (0, 1) if second else (1, 0)
             finish(cot_gathers[micro], gather_base(micro))
-            finish(gather, 0)
+            if second or index > 0:
+                finish(gather, 0)
             need(block)
-            going = micro == 0 or not last
+            going = not second or not last
             for step in BACKWARD_ORDER:
                 if step == 'X':
                     block.backward(micro, env.cots.at[index % 2, micro])
-                    reduce_start(micro)
+                elif step == 'P':
+                    if index == 0 and not second:
+                        after_forward(len(blocks) - 1, 1)
+                        for peer in ring.peers:
+                            pl.semaphore_signal(env.turn, inc=1, device_id={'tp': peer}, device_id_type=MESH)
+                        pl.semaphore_wait(env.turn, len(ring.peers))
+                    reduce_start(micro, block.backward_partial)
                 elif step == 'E':
-                    if micro == 1:
-                        after_backward(index, 0)
-                    elif index == 0:
-                        after_forward(len(blocks) - 1, 1)
-                    else:
-                        after_backward(index - 1, 1)
-                    if going:
-                        cot_start(index + micro, other)
+                    if second:
+                        after_backward(index, 1)
+                    elif index > 0:
+                        after_backward(index - 1, 0)
                 elif step == 'f':
                     reduce_far(micro)
                 elif step == 'w':
-                    store(block, block.weights_near(micro))
+                    store(block, block.weights_near(second))
                     full_done(gather)
                     cot_gathers[micro].sent()
                 elif step == 'r':
@@ -576,7 +610,7 @@
                         relay(cot_gathers[other], gather_base(other))
                 elif step == 'V':
                     if going:
-                        gather = full_start(block if micro == 0 else back[index + 1], other)
+                        gather = full_start(back[index + 1] if second else block, other)
                 elif step == 'n':
                     reduce_near(micro)
                 elif step == 'R':
@@ -584,13 +618,13 @@
                 elif step == 'v':
                     if going:
                         relay(gather, 0)
-                elif micro == 1:
+                elif second:
                     store(block, block.weights_far([env.cots.at[index % 2, 0], env.cots.at[index % 2, 1]]))
                 elif index > 0 and not last:
                     for copy in stores.pop(back[index - 1], ()):
                         copy.wait()
                     loads[back[index + 1]] = load(back[index + 1])
-    after_backward(len(back) - 1, 1)
+    after_backward(len(back) - 1, 0)
 
     copies = []
     for index, peer in enumerate(others):
@@ -655,7 +689,7 @@
         def dma(count):
             return pltpu.SemaphoreType.DMA((count,))
 
-        copies = 3 * AG_COPIES + 2 * RS_COPIES
+        copies = 3 * AG_COPIES + 2 * HALVES * RS_COPIES
         scratch = {
             'layer_rows': bf16(layers, micros, rows, width), 'hidden_rows': bf16(layers, micros, rows, width),
             'cot_rows': bf16(2, micros, rows, width), 'qkv': bf16(layers, micros, seq_len, qkv_width),
@@ -664,14 +698,15 @@
             'grad_mix': bf16(seq_len, mix_width), 'grad_qkv': bf16(seq_len, qkv_width),
             'qkv_w': bf16(width, qkv_width), 'out_w': bf16(mix_width, width), 'gate_w': bf16(width, inner_width),
             'up_w': bf16(width, inner_width), 'down_w': bf16(inner_width, width),
+            'stage_qkv': bf16(width, qkv_width), 'stage_gate': bf16(width, inner_width), 'stage_up': bf16(width, inner_width),
             'acc_qkv': f32(width, qkv_width), 'acc_gate': f32(width, inner_width), 'acc_up': f32(width, inner_width),
-            'full': bf16(seq_len, width), 'cots': bf16(2, micros, seq_len, width), 'part': f32(micros, seq_len, width),
-            'from_partner': f32(micros, 4, rows, width), 'sums': f32(micros, 4, rows, width),
-            'via_left': f32(micros, rows // 2, width), 'via_right': f32(micros, rows // 2, width),
-            'in_left': f32(micros, rows, width), 'in_right': f32(micros, rows, width),
+            'full': bf16(seq_len, width), 'cots': bf16(2, micros, seq_len, width), 'part': f32(micros, HALVES, seq_len, width // HALVES),
+            'from_partner': f32(micros, HALVES, 4, rows, width // HALVES), 'sums': f32(micros, HALVES, 4, rows, width // HALVES),
+            'via_left': f32(micros, HALVES, rows // 2, width // HALVES), 'via_right': f32(micros, HALVES, rows // 2, width // HALVES),
+            'in_left': f32(micros, HALVES, rows, width // HALVES), 'in_right': f32(micros, HALVES, rows, width // HALVES),
             'gains': f32(2 * layers, width), 'gain_parts': f32(devices, 2 * layers, width),
             'load_sems': dma(5), 'store_sems': dma(5), 'send_sems': dma(copies), 'recv_sems': dma(copies),
-            'gain_send': dma(devices - 1), 'gain_recv': dma(devices - 1), 'credit': pltpu.SemaphoreType.REGULAR}
+            'gain_send': dma(devices - 1), 'gain_recv': dma(devices - 1), 'credit': pltpu.SemaphoreType.REGULAR, 'turn': pltpu.SemaphoreType.REGULAR}
         names = (*inputs, *outputs, *scratch)
         sizes = dict(layers=layers, devices=devices, groups=groups, head_dim=head_dim)
         results = pl.pallas_call(

time: 367 us -> 346 us (0.943)
  Pallas kernels: 335 us -> 314 us
    pallas_call x1, Pallas kernels: 335 us -> 314 us  [device_program(): pl.pallas_call(functools.partial(stack_kernel, names, sizes), out_shape=t...]
where the time goes in v3:
time: 346 us; the launch traced here: 345 us
  Pallas kernels  314 us (91%)
  local copies, waits for them, and re-layouts  30.7 us (9%)
    pallas_call x1, Pallas kernels, device_program(): pl.pallas_call(functools.partial(stack_kernel, names, sizes), out_shape=t...  314 us
    unnamed x20, local copies, waits for them, and re-layouts  15.1 us
    reshape x1, local copies, waits for them, and re-layouts, device_program(): w_qkv.reshape(layers, width, qkv_width)  7.17 us

profile of v3, /device:TPU:81, one launch (start us, length us, event | category | flops | bytes accessed | tf_op | source)
XLA Modules:
  0.0 345.1 jit_solution(10820304897901230684)
XLA Ops:
  0.6 7.2 %reshape.30.refs_4_ = bf16[2,2048,512]{2,1,0:T(8,128)(2,1)} reshape(bf16[2,2048,1,4,128]{4,3,2,1,0:T(4,128)(2,1)} %param.13) | data formatting | bytes 8388608 | tf_op jit(solution)/shard_map/reshape | solution.py:671
  7.8 313.7 %stack.1 = (bf16[2,32,2048]{2,1,0:T(8,128)(2,1)}, bf16[2,32,2048]{2,1,0:T(8,128)(2,1)}, bf16[2,2048,512]{2,1,0:T(8,128)(2,1)}, bf16[2,256,2048]{2,1,0:T(8,128)(2...) custom-call(bf16[2,32,2048]{2,1,0:T(8,128)(2,1)} %refs_0_.1, ...), custom_call_target="tpu_custom_call" | custom-call | tf_op jit(solution)/shard_map/stack/pallas_call | solution.py:712
  321.5 0.0 copy-start.2
  321.5 0.0 copy-start.1
  321.6 0.0 copy-start
  321.6 1.5 fusion
  323.1 6.9 %reshape.32 = bf16[2,2048,1,4,128]{4,3,1,0,2:T(4,128)(2,1)} reshape(bf16[2,2048,512]{2,1,0:T(8,128)(2,1)} %get-tuple-element.19) | data formatting | bytes 8388608 | tf_op jit(solution)/shard_map/reshape | solution.py:719
  330.0 0.0 copy-done.2
  330.0 0.7 copy.25
  330.7 0.0 copy-done.1
  330.7 0.7 copy.26
  331.4 0.0 copy-done
  331.4 0.0 slice-start.2
  331.4 1.3 copy.27
  332.7 0.0 slice-start.3
  332.7 0.0 slice-start
  332.7 6.6 %copy.28 = bf16[2,2048,768]{2,1,0:T(8,128)(2,1)} copy(bf16[2,2048,768]{2,1,0:T(8,128)(2,1)} %get-tuple-element.49) | data formatting | bytes 12582912
  339.3 0.0 slice-done.2
  339.3 0.0 slice-done.3
  339.3 0.0 slice-start.1
  339.3 2.8 copy.29
  342.2 0.0 slice-done
  342.2 0.3 slice-done.1
  342.4 2.7 copy.30
  (2 shorter events, 0.0 us)
Async XLA Ops:
  321.5 8.5 %copy-start.2 = (bf16[2,32,2048]{2,1,0:T(8,128)(2,1)S(1)}, bf16[2,32,2048]{2,1,0:T(8,128)(2,1)}, u32[]{:S(2)}) copy-start(bf16[2,32,2048]{2,1,0:T(8,128)(2,1)} %get-tuple-element.45) | copy-start | bytes 786436
  321.5 9.2 %copy-start.1 = (bf16[2,32,2048]{2,1,0:T(8,128)(2,1)S(1)}, bf16[2,32,2048]{2,1,0:T(8,128)(2,1)}, u32[]{:S(2)}) copy-start(bf16[2,32,2048]{2,1,0:T(8,128)(2,1)} %get-tuple-element.46) | copy-start | bytes 786436
  321.6 9.9 %copy-start = (bf16[2,256,2048]{2,1,0:T(8,128)(2,1)S(1)}, bf16[2,256,2048]{2,1,0:T(8,128)(2,1)}, u32[]{:S(2)}) copy-start(bf16[2,256,2048]{2,1,0:T(8,128)(2,1)} %get-tuple-element.20) | copy-start | bytes 6291460
  331.4 7.9 %slice-start.2 = ((s8[6291456]{0:T(1024)(128)(4,1)}), s8[4194304]{0:T(1024)(128)(4,1)S(1)}, s32[]{:S(2)}) async-start(s8[6291456]{0:T(1024)(128)(4,1)} %bitcast.5), calls=%async_computation.2 | async-start | bytes 8388608
  332.7 6.6 %slice-start.3 = ((s8[6291456]{0:T(1024)(128)(4,1)}), s8[2097152]{0:T(1024)(128)(4,1)S(1)}, s32[]{:S(2)}) async-start(s8[6291456]{0:T(1024)(128)(4,1)} %bitcast.5), calls=%async_computation.3 | async-start | bytes 4194304
  332.7 9.4 %slice-start = ((s8[6291456]{0:T(1024)(128)(4,1)}), s8[4194304]{0:T(1024)(128)(4,1)S(1)}, s32[]{:S(2)}) async-start(s8[6291456]{0:T(1024)(128)(4,1)} %bitcast.3), calls=%async_computation | async-start | bytes 8388608
  339.3 3.1 slice-start.1
